TPU v7x, 512 devices: a 8x2x16 block of a 8x8x16 slice. The times are simulated.
512 devices in a mesh: groups: 2 (over y), section: 16 (over z), seq: 16 (over x, core).
Axes of the slice: x: 8, y: 2, z: 16, core: 2. Of those that a mesh axis runs over, the one named last changes fastest.
The devices are a block of a 8x8x16 slice.
Arguments:
- tokens: bfloat16 [8, 1024, 1440], P('groups', 'seq'), parts along dimension 0, may hold values from -6 to 6
- block_order: int32 [8], P('groups'), parts along dimension 0, may hold values from 0 to 3, each once
- prompt_lengths: int32 [8], P('groups'), parts along dimension 0, may hold values from 1 to 1024, 2304 in all
- norm_gain: float32 [16, 1440], P('section'), may hold values from 0.1 to 1.9
- w_query: bfloat16 [16, 1440, 2048], P('section', None, 'seq'), may hold values from -4 to 4
- w_key_value: bfloat16 [16, 1440, 512], P('section'), may hold values from -4 to 4
- w_out: bfloat16 [16, 2048, 1440], P('section', 'seq'), may hold values from -0.125 to 0.125
- sink_logits: float32 [16, 32], P('section'), may hold values from 0 to 4
Outputs:
- hidden_states: bfloat16 [16, 8, 1024, 1440], P('section', 'groups', 'seq'), parts along dimension 1
- layer_cache: bfloat16 [16, 8, 1024, 512], P('section', 'groups', 'seq'), parts along dimension 1
There are 2 independent parts, one for each index of `groups`. A program takes and returns all parts, laid end to end along the dimension named above; an argument that names none is the same for every part. Nothing has to cross between parts.
Inputs may be any that keep to these rules, and one draw needn't show every extreme that they name: `block_order`: each of 0 to 3 exactly once. `prompt_lengths`: the longest prompt is full.
All inputs are finite; a program needn't handle non-finite values.
Results may differ from a plain program's by a relative error of at most 0.024.
Values may be sent and summed in bfloat16 or wider, within the bound.
A program may use at most 128 MiB of HBM per device.

v0:
```python
import math

import jax
import jax.numpy as jnp
from jax import lax
from jax.sharding import PartitionSpec as P

HEAD_DIM = 64
WIN = 128


THETA = 150000.0
EPSILON = 1e-05


def rows_first(arrays, axis, dims):
    turned = [jnp.moveaxis(a, dim, 0) for a, dim in zip(arrays, dims)]
    widths = [t[0].size for t in turned]
    both = jnp.concatenate([t.reshape(-1, w) for t, w in zip(turned, widths)], axis=1)
    out = lax.all_gather(both, axis, axis=0, tiled=True)
    parts = jnp.split(out, [sum(widths[:k]) for k in range(1, len(widths))], axis=1)
    return tuple(
        (
            jnp.moveaxis(b.reshape(-1, *t.shape[1:]), 0, dim)
            for b, t, dim in zip(parts, turned, dims)
        )
    )


def from_behind(block, axis, distance):
    devices = range(lax.axis_size(axis))
    route = [(i - distance, i) for i in devices if i - distance in devices]
    return lax.ppermute(block, axis, route)


def rotary(positions, head_size):
    half = head_size // 2
    freq = jnp.exp(jnp.arange(half, dtype=jnp.float32) * (-2.0 * math.log(THETA) / head_size))
    angles = positions.astype(jnp.float32)[:, None] * freq[None, :]
    return (jnp.cos(angles)[:, None, :], jnp.sin(angles)[:, None, :])


def rotate(values, cosine, sine):
    half = values.shape[-1] // 2
    first = values[..., :half]
    second = values[..., half:]
    return jnp.concatenate([first * cosine - second * sine, second * cosine + first * sine], -1)


def per_device(
    tokens, block_order, prompt_lengths, norm_gain, w_query, w_key_value, w_out, sink_logits
):
    section_index = lax.axis_index("section")
    sections = lax.axis_size("section")
    seq_index = lax.axis_index("seq")
    micro, rows, width = tokens.shape
    full_query, full_out = rows_first((w_query, w_out), "seq", (2, 1))
    query_weight = full_query[0]
    out_weight = full_out[0]
    pair_weight = w_key_value[0]
    gain = norm_gain[0]
    heads_width = query_weight.shape[1]
    head_count = heads_width // HEAD_DIM
    kv_width = pair_weight.shape[1] // 2
    kv_heads = kv_width // HEAD_DIM
    group = head_count // kv_heads
    sink = sink_logits[0].reshape(kv_heads, group)[:, :, None]
    keep = min(WIN, rows)
    depth = WIN // keep
    start = seq_index * rows
    positions = start + jnp.arange(rows, dtype=jnp.int32)
    cosine, sine = rotary(positions, HEAD_DIM)
    key_positions = start - WIN + jnp.arange(WIN + rows, dtype=jnp.int32)

    def project(hidden):
        widened = hidden.astype(jnp.float32)
        scale = lax.rsqrt(jnp.mean(widened * widened, -1, keepdims=True) + EPSILON)
        normed = (widened * scale * gain).astype(jnp.bfloat16)
        queries = jnp.dot(normed, query_weight, preferred_element_type=jnp.float32).reshape(
            rows, head_count, HEAD_DIM
        )
        queries = rotate(queries, cosine, sine).astype(jnp.bfloat16).reshape(rows, heads_width)
        projected = jnp.dot(normed, pair_weight, preferred_element_type=jnp.float32)
        rotated = rotate(
            projected[:, :kv_width].reshape(rows, kv_heads, HEAD_DIM), cosine, sine
        ).reshape(rows, kv_width)
        cache = jnp.concatenate([rotated, projected[:, kv_width:]], 1).astype(jnp.bfloat16)
        return (queries, cache)

    def project_spare(hidden):
        return (
            jnp.zeros((rows, heads_width), jnp.bfloat16),
            jnp.zeros((rows, 2 * kv_width), jnp.bfloat16),
        )

    def window_of(cache):
        pieces = [from_behind(cache, "seq", offset) for offset in range(depth, 0, -1)]
        return jnp.concatenate(pieces, 0)

    def attend(operands):
        hidden, queries, cache, window, length = operands
        joined = jnp.concatenate([window, cache], 0)
        key_heads = joined[:, :kv_width].reshape(WIN + rows, kv_heads, HEAD_DIM)
        value_heads = joined[:, kv_width:].reshape(WIN + rows, kv_heads, HEAD_DIM)
        grouped = queries.reshape(rows, kv_heads, group, HEAD_DIM)
        scores = (
            jnp.einsum("qkgd,skd->kgqs", grouped, key_heads, preferred_element_type=jnp.float32)
            * 0.125
        )
        query_col = positions[:, None]
        key_row = key_positions[None, :]
        allowed = (key_row <= query_col) & (query_col - key_row < WIN) & (key_row >= 0)
        allowed = allowed & ((key_row < length) | (key_row == query_col))
        masked = jnp.where(allowed, scores, jnp.float32(-1e30))
        top = jnp.maximum(jnp.max(masked, -1), sink)
        expo = jnp.where(allowed, jnp.exp(scores - top[..., None]), jnp.float32(0.0))
        total = jnp.sum(expo, -1) + jnp.exp(sink - top)
        weights = (expo / total[..., None]).astype(jnp.bfloat16)
        context = jnp.einsum(
            "kgqs,skd->qkgd", weights, value_heads, preferred_element_type=jnp.float32
        )
        context = context.reshape(rows, heads_width).astype(jnp.bfloat16)
        output = jnp.dot(context, out_weight, preferred_element_type=jnp.float32)
        return (hidden.astype(jnp.float32) + output).astype(jnp.bfloat16)

    def pass_through(operands):
        return operands[0]

    def turn(counter, carry):
        arriving, hidden_buffer, cache_buffer = carry
        slot = counter - section_index
        active = (slot >= 0) & (slot < micro)
        slot_safe = jnp.clip(slot, 0, micro - 1)
        block = block_order[slot_safe]
        length = prompt_lengths[block]
        entering = lax.dynamic_index_in_dim(tokens, block, 0, keepdims=False)
        hidden = jnp.where(section_index == 0, entering, arriving)
        queries, cache = lax.cond(active, project, project_spare, hidden)
        window = window_of(cache)
        updated = lax.cond(active, attend, pass_through, (hidden, queries, cache, window, length))
        previous_hidden = lax.dynamic_index_in_dim(hidden_buffer, slot_safe, 0, keepdims=False)
        previous_cache = lax.dynamic_index_in_dim(cache_buffer, slot_safe, 0, keepdims=False)
        hidden_buffer = lax.dynamic_update_index_in_dim(
            hidden_buffer, jnp.where(active, updated, previous_hidden), slot_safe, 0
        )
        cache_buffer = lax.dynamic_update_index_in_dim(
            cache_buffer, jnp.where(active, cache, previous_cache), slot_safe, 0
        )
        passed = from_behind(updated, "section", 1)
        return (passed, hidden_buffer, cache_buffer)

    initial = (
        jnp.zeros((rows, width), jnp.bfloat16),
        jnp.zeros((micro, rows, width), jnp.bfloat16),
        jnp.zeros((micro, rows, 2 * kv_width), jnp.bfloat16),
    )
    final = lax.fori_loop(0, micro + sections - 1, turn, initial)
    return (final[1][None], final[2][None])


def solution(mesh):
    in_specs = (
        P("groups", "seq", None),
        P("groups"),
        P("groups"),
        P("section", None),
        P("section", None, "seq"),
        P("section", None, None),
        P("section", "seq", None),
        P("section", None),
    )
    out_specs = (P("section", "groups", "seq", None), P("section", "groups", "seq", None))
    return jax.shard_map(
        per_device, mesh=mesh, in_specs=in_specs, out_specs=out_specs, check_vma=False
    )
```

profile of v0, /device:TPU:1858, one launch (start us, length us, event | category | flops | bytes accessed | tf_op | source)
XLA Modules:
  0.0 783.1 jit_solution(16255271315744415141)
XLA Ops:
  10.6 83.0 %all-gather.2.cloned.1.call-done = bf16[2048,2880]{0,1:T(8,128)(2,1)} async-done(((bf16[128,2880]{0,1:T(8,128)(2,1)}), bf16[2048,2880]{0,1:T(8,128)(2,1)}) %all-gather.2.cloned.1.call-update) | async-done | bytes 11796496 | tf_op jit(solution)/shard_map/all_gather | solution.py:20
  93.6 10.2 %fusion.29 = (bf16[2048,1440]{0,1:T(8,128)(2,1)}, bf16[1440,2048]{1,0:T(8,128)(2,1)}) fusion(bf16[2048,2880]{0,1:T(8,128)(2,1)} %all-gather.2.cloned.1.call-done), kind=kLoop, calls=%fused_computation.61 | loop fusion | bytes 23592960 | tf_op jit(solution)/shard_map/split | solution.py:21
  103.8 8.7 %copy.20 = bf16[2048,1440]{1,0:T(8,128)(2,1)} copy(bf16[2048,1440]{0,1:T(8,128)(2,1)} %get-tuple-element.613) | data formatting | bytes 11796480
  114.2 662.0 %while.20 = (s32[]{:T(128)}, bf16[64,1440]{1,0:T(8,128)(2,1)S(1)}, bf16[4,64,1440]{2,1,0:T(8,128)(2,1)}, bf16[4,64,512]{2,1,0:T(8,128)(2,1)}, s32[]{:T(128)}, /*...) while((s32[]{:T(128)}, bf16[64,1440]{1,0:T(8,128)(2,1)S(1)}, ...), condition=%wide.region_8.9_spmd.clone.clone, body=%wide.region_0.8_spmd.clone.clone.sunk | while | flops 958372544 | bytes 48405112 | solution.py:157
  131.1 4.2 collective-permute-done.2
  139.3 3.4 collective-permute-start
  152.7 4.2 collective-permute-done.2
  160.9 4.0 collective-permute-start
  174.8 4.3 collective-permute-done.2
  183.1 3.7 collective-permute-start
  196.7 5.5 collective-permute-done.2
  206.1 3.2 collective-permute-start
  218.5 6.1 collective-permute-done.2
  228.6 3.2 collective-permute-start
  241.0 6.1 collective-permute-done.2
  251.2 3.2 collective-permute-start
  263.5 6.1 collective-permute-done.2
  273.7 3.2 collective-permute-start
  286.1 6.1 collective-permute-done.2
  296.2 3.2 collective-permute-start
  308.6 6.1 collective-permute-done.2
  318.7 3.2 collective-permute-start
  331.1 6.1 collective-permute-done.2
  353.6 6.1 collective-permute-done.2
  376.1 6.1 collective-permute-done.2
  398.6 6.1 collective-permute-done.2
  421.1 176.7 %collective-permute-done.2 = bf16[64,1440]{1,0:T(8,128)(2,1)S(1)} collective-permute-done((bf16[64,1440]{1,0:T(8,128)(2,1)S(1)}, bf16[64,1440]{1,0:T(8,128)(2,1)S(1)}, u32[]{:S(2)}, u32[]{:S(2)}) %collective-permute-start.2) | collective-permute-done | bytes 184352 | tf_op jit(solution)/shard_map/while/body/eval_jaxpr/ppermute | solution.py:33
  601.1 7.7 conditional.8
  603.3 3.9 fusion.26
  608.9 3.2 collective-permute-start
  618.6 7.1 conditional.9
  628.4 6.1 collective-permute-done.2
  637.8 7.7 conditional.8
  640.0 3.9 fusion.26
  645.5 3.2 collective-permute-start
  655.2 7.1 conditional.9
  665.0 6.1 collective-permute-done.2
  674.5 7.7 conditional.8
  676.6 3.9 fusion.26
  682.2 3.2 collective-permute-start
  691.9 7.1 conditional.9
  701.7 6.1 collective-permute-done.2
  711.1 7.7 conditional.8
  713.3 3.9 fusion.26
  718.8 3.2 collective-permute-start
  728.6 7.1 conditional.9
  738.3 4.9 collective-permute-done.2
  756.7 16.4 %collective-permute-start.2 = (bf16[64,1440]{1,0:T(8,128)(2,1)S(1)}, bf16[64,1440]{1,0:T(8,128)(2,1)S(1)}, u32[]{:S(2)}, u32[]{:S(2)}) collective-permute-start(bf16[64,1440]{1,0:T(8,128)(2,1)S(1)} %get-tuple-element.802), channel_id=1, source_target_pairs={{0,16},{16,32},{32,48},{48,64},{64,80},{80,96},{96,112},{112,128},... | collective-permute-start | bytes 552968 | tf_op jit(solution)/shard_map/while/body/eval_jaxpr/ppermute | solution.py:33
  (513 shorter events, 295.8 us)
Async XLA Ops:
  7.2 86.4 %all-gather.2.cloned.1.call-start = ((), (), s32[]{:S(2)}) async-start(), calls=%async_computation | async-start | bytes 12533760 | tf_op jit(solution)/shard_map/all_gather | solution.py:20
  118.3 7.8 collective-permute-start
  121.2 6.5 collective-permute-start.1
  127.7 7.6 collective-permute-start.2
  139.3 7.8 collective-permute-start
  142.8 6.5 collective-permute-start.1
  149.3 7.6 collective-permute-start.2
  160.9 8.4 %collective-permute-start = (bf16[64,512]{0,1:T(8,128)(2,1)}, bf16[64,512]{0,1:T(8,128)(2,1)S(1)}, u32[]{:S(2)}, u32[]{:S(2)}) collective-permute-start(bf16[64,512]{0,1:T(8,128)(2,1)} %get-tuple-element.727), channel_id=1, source_target_pairs={{0,2},{1,3},{2,4},{3,5},{4,6},{5,7},{6,8},{7,9},{8,10},{9,11},{10,... | collective-permute-start | bytes 196616 | tf_op jit(solution)/shard_map/while/body/eval_jaxpr/ppermute | solution.py:33
  164.9 6.5 collective-permute-start.1
  171.4 7.7 collective-permute-start.2
  183.1 8.1 %collective-permute-start = (bf16[64,512]{0,1:T(8,128)(2,1)}, bf16[64,512]{0,1:T(8,128)(2,1)S(1)}, u32[]{:S(2)}, u32[]{:S(2)}) collective-permute-start(bf16[64,512]{0,1:T(8,128)(2,1)} %get-tuple-element.727), channel_id=1, source_target_pairs={{0,2},{1,3},{2,4},{3,5},{4,6},{5,7},{6,8},{7,9},{8,10},{9,11},{10,... | collective-permute-start | bytes 196616 | tf_op jit(solution)/shard_map/while/body/eval_jaxpr/ppermute | solution.py:33
  186.8 6.5 collective-permute-start.1
  193.3 8.8 %collective-permute-start.2 = (bf16[64,1440]{1,0:T(8,128)(2,1)S(1)}, bf16[64,1440]{1,0:T(8,128)(2,1)S(1)}, u32[]{:S(2)}, u32[]{:S(2)}) collective-permute-start(bf16[64,1440]{1,0:T(8,128)(2,1)S(1)} %get-tuple-element.802), channel_id=1, source_target_pairs={{0,16},{16,32},{32,48},{48,64},{64,80},{80,96},{96,112},{112,128},... | collective-permute-start | bytes 552968 | tf_op jit(solution)/shard_map/while/body/eval_jaxpr/ppermute | solution.py:33
  206.1 7.6 collective-permute-start
  209.3 6.5 collective-permute-start.1
  215.8 8.8 %collective-permute-start.2 = (bf16[64,1440]{1,0:T(8,128)(2,1)S(1)}, bf16[64,1440]{1,0:T(8,128)(2,1)S(1)}, u32[]{:S(2)}, u32[]{:S(2)}) collective-permute-start(bf16[64,1440]{1,0:T(8,128)(2,1)S(1)} %get-tuple-element.802), channel_id=1, source_target_pairs={{0,16},{16,32},{32,48},{48,64},{64,80},{80,96},{96,112},{112,128},... | collective-permute-start | bytes 552968 | tf_op jit(solution)/shard_map/while/body/eval_jaxpr/ppermute | solution.py:33
  228.6 7.6 collective-permute-start
  238.4 8.8 %collective-permute-start.2 = (bf16[64,1440]{1,0:T(8,128)(2,1)S(1)}, bf16[64,1440]{1,0:T(8,128)(2,1)S(1)}, u32[]{:S(2)}, u32[]{:S(2)}) collective-permute-start(bf16[64,1440]{1,0:T(8,128)(2,1)S(1)} %get-tuple-element.802), channel_id=1, source_target_pairs={{0,16},{16,32},{32,48},{48,64},{64,80},{80,96},{96,112},{112,128},... | collective-permute-start | bytes 552968 | tf_op jit(solution)/shard_map/while/body/eval_jaxpr/ppermute | solution.py:33
  251.2 7.6 collective-permute-start
  260.9 8.8 %collective-permute-start.2 = (bf16[64,1440]{1,0:T(8,128)(2,1)S(1)}, bf16[64,1440]{1,0:T(8,128)(2,1)S(1)}, u32[]{:S(2)}, u32[]{:S(2)}) collective-permute-start(bf16[64,1440]{1,0:T(8,128)(2,1)S(1)} %get-tuple-element.802), channel_id=1, source_target_pairs={{0,16},{16,32},{32,48},{48,64},{64,80},{80,96},{96,112},{112,128},... | collective-permute-start | bytes 552968 | tf_op jit(solution)/shard_map/while/body/eval_jaxpr/ppermute | solution.py:33
  273.7 7.6 collective-permute-start
  276.8 6.5 collective-permute-start.1
  283.4 8.8 %collective-permute-start.2 = (bf16[64,1440]{1,0:T(8,128)(2,1)S(1)}, bf16[64,1440]{1,0:T(8,128)(2,1)S(1)}, u32[]{:S(2)}, u32[]{:S(2)}) collective-permute-start(bf16[64,1440]{1,0:T(8,128)(2,1)S(1)} %get-tuple-element.802), channel_id=1, source_target_pairs={{0,16},{16,32},{32,48},{48,64},{64,80},{80,96},{96,112},{112,128},... | collective-permute-start | bytes 552968 | tf_op jit(solution)/shard_map/while/body/eval_jaxpr/ppermute | solution.py:33
  296.2 7.6 collective-permute-start
  299.4 6.5 collective-permute-start.1
  305.9 8.8 %collective-permute-start.2 = (bf16[64,1440]{1,0:T(8,128)(2,1)S(1)}, bf16[64,1440]{1,0:T(8,128)(2,1)S(1)}, u32[]{:S(2)}, u32[]{:S(2)}) collective-permute-start(bf16[64,1440]{1,0:T(8,128)(2,1)S(1)} %get-tuple-element.802), channel_id=1, source_target_pairs={{0,16},{16,32},{32,48},{48,64},{64,80},{80,96},{96,112},{112,128},... | collective-permute-start | bytes 552968 | tf_op jit(solution)/shard_map/while/body/eval_jaxpr/ppermute | solution.py:33
  318.7 7.6 collective-permute-start
  321.9 6.5 collective-permute-start.1
  328.4 8.8 %collective-permute-start.2 = (bf16[64,1440]{1,0:T(8,128)(2,1)S(1)}, bf16[64,1440]{1,0:T(8,128)(2,1)S(1)}, u32[]{:S(2)}, u32[]{:S(2)}) collective-permute-start(bf16[64,1440]{1,0:T(8,128)(2,1)S(1)} %get-tuple-element.802), channel_id=1, source_target_pairs={{0,16},{16,32},{32,48},{48,64},{64,80},{80,96},{96,112},{112,128},... | collective-permute-start | bytes 552968 | tf_op jit(solution)/shard_map/while/body/eval_jaxpr/ppermute | solution.py:33
  341.2 7.6 collective-permute-start
  344.4 6.5 collective-permute-start.1
  350.9 8.8 %collective-permute-start.2 = (bf16[64,1440]{1,0:T(8,128)(2,1)S(1)}, bf16[64,1440]{1,0:T(8,128)(2,1)S(1)}, u32[]{:S(2)}, u32[]{:S(2)}) collective-permute-start(bf16[64,1440]{1,0:T(8,128)(2,1)S(1)} %get-tuple-element.802), channel_id=1, source_target_pairs={{0,16},{16,32},{32,48},{48,64},{64,80},{80,96},{96,112},{112,128},... | collective-permute-start | bytes 552968 | tf_op jit(solution)/shard_map/while/body/eval_jaxpr/ppermute | solution.py:33
  363.7 7.6 collective-permute-start
  373.4 8.8 %collective-permute-start.2 = (bf16[64,1440]{1,0:T(8,128)(2,1)S(1)}, bf16[64,1440]{1,0:T(8,128)(2,1)S(1)}, u32[]{:S(2)}, u32[]{:S(2)}) collective-permute-start(bf16[64,1440]{1,0:T(8,128)(2,1)S(1)} %get-tuple-element.802), channel_id=1, source_target_pairs={{0,16},{16,32},{32,48},{48,64},{64,80},{80,96},{96,112},{112,128},... | collective-permute-start | bytes 552968 | tf_op jit(solution)/shard_map/while/body/eval_jaxpr/ppermute | solution.py:33
  386.2 7.6 collective-permute-start
  395.9 8.8 %collective-permute-start.2 = (bf16[64,1440]{1,0:T(8,128)(2,1)S(1)}, bf16[64,1440]{1,0:T(8,128)(2,1)S(1)}, u32[]{:S(2)}, u32[]{:S(2)}) collective-permute-start(bf16[64,1440]{1,0:T(8,128)(2,1)S(1)} %get-tuple-element.802), channel_id=1, source_target_pairs={{0,16},{16,32},{32,48},{48,64},{64,80},{80,96},{96,112},{112,128},... | collective-permute-start | bytes 552968 | tf_op jit(solution)/shard_map/while/body/eval_jaxpr/ppermute | solution.py:33
  408.8 7.6 collective-permute-start
  418.5 179.4 %collective-permute-start.2 = (bf16[64,1440]{1,0:T(8,128)(2,1)S(1)}, bf16[64,1440]{1,0:T(8,128)(2,1)S(1)}, u32[]{:S(2)}, u32[]{:S(2)}) collective-permute-start(bf16[64,1440]{1,0:T(8,128)(2,1)S(1)} %get-tuple-element.802), channel_id=1, source_target_pairs={{0,16},{16,32},{32,48},{48,64},{64,80},{80,96},{96,112},{112,128},... | collective-permute-start | bytes 552968 | tf_op jit(solution)/shard_map/while/body/eval_jaxpr/ppermute | solution.py:33
  608.9 7.6 collective-permute-start
  625.7 8.8 %collective-permute-start.2 = (bf16[64,1440]{1,0:T(8,128)(2,1)S(1)}, bf16[64,1440]{1,0:T(8,128)(2,1)S(1)}, u32[]{:S(2)}, u32[]{:S(2)}) collective-permute-start(bf16[64,1440]{1,0:T(8,128)(2,1)S(1)} %get-tuple-element.802), channel_id=1, source_target_pairs={{0,16},{16,32},{32,48},{48,64},{64,80},{80,96},{96,112},{112,128},... | collective-permute-start | bytes 552968 | tf_op jit(solution)/shard_map/while/body/eval_jaxpr/ppermute | solution.py:33
  645.5 7.6 collective-permute-start
  662.4 8.8 %collective-permute-start.2 = (bf16[64,1440]{1,0:T(8,128)(2,1)S(1)}, bf16[64,1440]{1,0:T(8,128)(2,1)S(1)}, u32[]{:S(2)}, u32[]{:S(2)}) collective-permute-start(bf16[64,1440]{1,0:T(8,128)(2,1)S(1)} %get-tuple-element.802), channel_id=1, source_target_pairs={{0,16},{16,32},{32,48},{48,64},{64,80},{80,96},{96,112},{112,128},... | collective-permute-start | bytes 552968 | tf_op jit(solution)/shard_map/while/body/eval_jaxpr/ppermute | solution.py:33
  682.2 7.6 collective-permute-start
  699.0 8.8 %collective-permute-start.2 = (bf16[64,1440]{1,0:T(8,128)(2,1)S(1)}, bf16[64,1440]{1,0:T(8,128)(2,1)S(1)}, u32[]{:S(2)}, u32[]{:S(2)}) collective-permute-start(bf16[64,1440]{1,0:T(8,128)(2,1)S(1)} %get-tuple-element.802), channel_id=1, source_target_pairs={{0,16},{16,32},{32,48},{48,64},{64,80},{80,96},{96,112},{112,128},... | collective-permute-start | bytes 552968 | tf_op jit(solution)/shard_map/while/body/eval_jaxpr/ppermute | solution.py:33
  718.8 7.6 collective-permute-start
  735.7 7.6 collective-permute-start.2
  747.3 7.3 collective-permute-start
  756.7 19.5 %collective-permute-start.2 = (bf16[64,1440]{1,0:T(8,128)(2,1)S(1)}, bf16[64,1440]{1,0:T(8,128)(2,1)S(1)}, u32[]{:S(2)}, u32[]{:S(2)}) collective-permute-start(bf16[64,1440]{1,0:T(8,128)(2,1)S(1)} %get-tuple-element.802), channel_id=1, source_target_pairs={{0,16},{16,32},{32,48},{48,64},{64,80},{80,96},{96,112},{112,128},... | collective-permute-start | bytes 552968 | tf_op jit(solution)/shard_map/while/body/eval_jaxpr/ppermute | solution.py:33
  (31 other events, 150.7 us)
Sparse Core Ops, SparseCore 0:
  10.7 82.9 all-gather.1
where the time goes:
time: 788 us; the launch traced here: 783 us
  waiting for transfers between devices  399 us (51%)
  starting transfers between devices  153 us (19%)
  local copies, waits for them, and re-layouts  94.3 us (12%)
  other arithmetic  60.3 us (8%)
  loops' own time  34.1 us (4%)
  matrix products  28.7 us (4%)
  between operations  14.1 us (2%)
    ppermute x57, waiting for transfers between devices, from_behind(): return lax.ppermute(block, axis, route)  316 us
    ppermute x57, starting transfers between devices, from_behind(): return lax.ppermute(block, axis, route)  152 us
    all_gather x1, waiting for transfers between devices, rows_first(): out = lax.all_gather(both, axis, axis=0, tiled=True)  83 us
    another operation x1, loops' own time, per_device(): final = lax.fori_loop(0, micro + sections - 1, turn, initial)  32.9 us
    select_n x19, other arithmetic, turn(): hidden = jnp.where(section_index == 0, entering, arriving)  18.1 us
    dynamic_slice x19, local copies, waits for them, and re-layouts, turn(): lax.dynamic_index_in_dim(hidden_buffer, slot_safe, 0, keepdims=False)  18 us
    dynamic_slice x19, local copies, waits for them, and re-layouts, turn(): lax.dynamic_index_in_dim(cache_buffer, slot_safe, 0, keepdims=False)  16.2 us
  transfers between devices with their start and end apart: 58, of which 40 were waited for; matrix products, arithmetic and copies ran while one was open for 8% of the time, Pallas kernels for 0%

commit v1 on v0

v1 whole, which is shorter than its diff:
```python
import functools
import math

import jax
import jax.numpy as jnp
from jax import lax
from jax.experimental import pallas as pl
from jax.experimental.pallas import tpu as pltpu
from jax.sharding import PartitionSpec as P

MESH = pl.DeviceIdType.MESH
HEAD_DIM = 64
HALF = HEAD_DIM // 2
WIN = 128
TILE = 256
THETA = 150000.0
EPSILON = 1e-05
LOW = -1e30
F32 = jnp.float32
BF16 = jnp.bfloat16


def dot(a, b):
    return jnp.dot(a, b, preferred_element_type=F32)


def kernel(
    seqs, sections, micro, width,
    wq_in, wkv_in, wo_in, tok_in, cos_in, sin_in, sink_in, length_in,
    hid_out, cache_out,
    wq, wo, h, tok, kv_acc, q_acc, q, kv_own, kv_prev, ctx, o_acc, h_new, stage_h, stage_v,
    wq_recv, wq_own, wq_relay, wo_recv, wo_own, wo_relay,
    tok_send, tok_recv, h_send, h_recv, f_send, f_recv, kv_send, kv_recv, c_send, c_recv,
    oh_local, oh_send, oh_recv, oc_local, oc_send, oc_recv,
):
    chips = seqs // 2
    half_chips = chips // 2
    shards = seqs // 2
    tiles = h.shape[1] // (2 * TILE)
    ctx_tiles = shards // 2
    me = lax.axis_index("seq")
    section = lax.axis_index("section")
    x = me // 2
    c = me % 2
    other = 1 - c
    partner = {"seq": 2 * x + other}

    def chip(step, core):
        return {"seq": 2 * ((x + step + chips) % chips) + core}

    def remote(src, dst, send, recv, target):
        return pltpu.make_async_remote_copy(
            src_ref=src, dst_ref=dst, send_sem=send, recv_sem=recv, device_id=target, device_id_type=MESH
        )

    up = {"section": (section + 1) % sections}
    down = {"section": (section + sections - 1) % sections}
    barrier = pltpu.get_barrier_semaphore()
    for target in (partner, chip(1, 0), chip(1, 1), chip(-1, 0), chip(-1, 1), up, down):
        pl.semaphore_signal(barrier, inc=1, device_id=target, device_id_type=MESH)
    pl.semaphore_wait(barrier, 7)

    home = x // half_chips

    def wq_slot(index):
        return wq.at[:, pl.ds(pl.multiple_of(128 * index, 128), 128), :]

    def wo_slot(owner, core):
        return wo.at[owner, :, pl.ds(pl.multiple_of(128 * core, 128), 128)]

    mine = me - shards * home

    def own_query(which, target):
        return remote(wq_in, wq_slot(mine), wq_own.at[which], wq_recv.at[mine], target)

    def local_query():
        return pltpu.make_async_copy(wq_in, wq_slot(mine), wq_recv.at[mine])

    def own_out(half, which, target):
        return remote(wo_in.at[half], wo_slot(x, c), wo_own.at[half, which], wo_recv.at[me], target)

    def local_out():
        return pltpu.make_async_copy(wo_in.at[c], wo_slot(x, c), wo_recv.at[me])

    own_query(0, chip(1, home)).start()
    own_query(1, chip(-1, home)).start()
    for half in range(2):
        own_out(half, 0, chip(1, half)).start()
        own_out(half, 1, chip(-1, half)).start()

    @pl.when(c == home)
    def _():
        local_query().start()

    @pl.when(c != home)
    def _():
        own_query(2, partner).start()

    local_out().start()
    remote(wo_in.at[other], wo_slot(x, c), wo_own.at[other, 2], wo_recv.at[me], partner).start()

    def query_copy(index, sign):
        return remote(wq_slot(index), wq_slot(index), wq_relay.at[index], wq_recv.at[index], chip(sign, c))

    def out_copy(owner, core, sign):
        slot = wo_slot(owner, core)
        return remote(slot, slot, wo_relay.at[2 * owner + core], wo_recv.at[2 * owner + core], chip(sign, c))

    def each_query(step, sign, hops, act):
        owner = (x - sign * step + chips) % chips

        @pl.when((step <= hops) & (owner // half_chips == c))
        def _():
            for core in range(2):
                act(query_copy(2 * owner + core - shards * c, sign), step < hops)

    def each_out(step, sign, hops, act):
        owner = (x - sign * step + chips) % chips

        @pl.when(step <= hops)
        def _():
            for core in range(2):
                act(out_copy(owner, core, sign), step < hops)

    def relay(copy, more):
        copy.wait_recv()

        @pl.when(more)
        def _():
            copy.start()

    def settle(copy, more):
        @pl.when(more)
        def _():
            copy.wait_send()

    def each_step(act):
        def body(step, carry):
            each_query(step, 1, half_chips, act)
            each_query(step, -1, half_chips - 1, act)
            each_out(step, -1, half_chips, act)
            each_out(step, 1, half_chips - 1, act)
            return carry

        lax.fori_loop(1, half_chips + 1, body, 0)

    rows = pl.ds(pl.multiple_of(64 * c, 64), 64)
    other_rows = pl.ds(pl.multiple_of(64 * other, 64), 64)

    def tok_remote():
        return remote(tok_in, tok.at[:, rows, :], tok_send, tok_recv.at[1], partner)

    def tok_local():
        return pltpu.make_async_copy(tok_in, tok.at[:, rows, :], tok_recv.at[0])

    @pl.when(section == 0)
    def _():
        tok_remote().start()
        tok_local().start()
        tok_local().wait()
        tok_remote().wait()

        def turn(slot, carry):
            for k in range(2 * tiles):
                piece = tok[slot, :, TILE * k : TILE * (k + 1)].astype(F32)
                h[slot, TILE * k : TILE * (k + 1), :] = piece.T.astype(BF16)
            return carry

        lax.fori_loop(0, micro, turn, 0)

    @pl.when(x == 0)
    def _():
        kv_prev[...] = jnp.zeros_like(kv_prev)

    each_step(relay)
    own_slot = wq_slot(2 * (x % half_chips))

    @pl.when(c == home)
    def _():
        for core in range(2):
            index = 2 * x + core - shards * c
            pltpu.make_async_copy(wq_in, wq_slot(index), wq_recv.at[index]).wait()

    for core in range(2):
        pltpu.make_async_copy(wo_in.at[0], wo_slot(x, core), wo_recv.at[2 * x + core]).wait()

    def h_tile(slot, k):
        return h.at[slot, pl.ds(pl.multiple_of(TILE * k, TILE), TILE), :]

    def pass_on(slot, k):
        return remote(h_new.at[slot, k], h_tile(slot, tiles * c + k), h_send.at[slot, k], h_recv.at[slot, k], up)

    def forward(slot, k, core):
        piece = h_tile(slot, tiles * core + k)
        return remote(piece, piece, f_send.at[slot, k], f_recv.at[slot, k], partner)

    def kv_copy(slot, which):
        return remote(
            kv_own.at[slot, which], kv_prev.at[slot, which], kv_send.at[slot, which], kv_recv.at[slot, which],
            chip(1, c),
        )

    def ctx_tile(core, m):
        return pl.ds(pl.multiple_of(TILE * (ctx_tiles * core + m), TILE), TILE)

    def ctx_copy(slot, core, m):
        piece = ctx.at[slot, ctx_tile(core, m), :]
        return remote(piece, piece, c_send.at[slot, m], c_recv.at[slot, m], partner)

    def hid_columns(core, k):
        return pl.ds(pl.multiple_of(TILE * (tiles * core + k), TILE), TILE)

    def hid_local(slot, k):
        return pltpu.make_async_copy(
            stage_h.at[slot, k, rows, :], hid_out.at[slot, :, hid_columns(c, k)], oh_local.at[slot, k]
        )

    def hid_remote(slot, k, core):
        return remote(
            stage_h.at[slot, k, other_rows, :], hid_out.at[slot, :, hid_columns(core, k)],
            oh_send.at[slot, k], oh_recv.at[slot, k], partner,
        )

    def cache_columns(core, which):
        return pl.ds(pl.multiple_of(256 * which + 128 * core, 128), 128)

    def cache_source(slot, which, span):
        return kv_own.at[slot, 0, span, :] if which == 0 else stage_v.at[slot, span, :]

    def cache_local(slot, which):
        return pltpu.make_async_copy(
            cache_source(slot, which, rows), cache_out.at[slot, :, cache_columns(c, which)], oc_local.at[slot, which]
        )

    def cache_remote(slot, which, core):
        return remote(
            cache_source(slot, which, other_rows), cache_out.at[slot, :, cache_columns(core, which)],
            oc_send.at[slot, which], oc_recv.at[slot, which], partner,
        )

    key = lax.broadcasted_iota(jnp.int32, (WIN, 128), 0)
    token = lax.broadcasted_iota(jnp.int32, (WIN, 128), 1)
    lower = key <= token
    lower_pair = jnp.concatenate([lower.astype(jnp.int32)] * 2, 1) == 1

    def one_slot(slot, carry):
        length = length_in[slot]
        allowed_own = (WIN * x + key < length) | (key == token)
        allowed_prev = (WIN * x - WIN + key < length) & (x > 0)
        bias = jnp.where(lower, jnp.where(allowed_own, 0.0, LOW), jnp.where(allowed_prev, 0.0, LOW))
        bias = jnp.concatenate([bias, bias], 1)

        kv_acc[...] = jnp.zeros_like(kv_acc)
        q_acc[...] = jnp.zeros_like(q_acc)
        squares = jnp.zeros((8, 128), F32)
        for k in range(tiles):
            for own in (True, False):
                core = c if own else other
                kt = tiles * core + k

                @pl.when(section > 0)
                def _():
                    if own:
                        pass_on(slot, k).wait_recv()
                        forward(slot, k, c).start()
                    else:
                        forward(slot, k, other).wait_recv()

                piece = h[slot, pl.ds(pl.multiple_of(TILE * kt, TILE), TILE), :]
                wide = piece.astype(F32)
                squares = squares + jnp.sum((wide * wide).reshape(TILE // 8, 8, 128), 0)
                kv_acc[...] += dot(wkv_in[kt], piece)
                if k < tiles - 1 or own:
                    q_acc[...] += dot(wq[kt], piece)
        scale = lax.rsqrt(jnp.sum(squares, 0, keepdims=True) * (1.0 / width) + EPSILON)
        cosine = cos_in[...] * scale
        sine = sin_in[...] * scale

        def rotate(first, second):
            return jnp.concatenate([first * cosine - second * sine, second * cosine + first * sine], 0)

        keys = jnp.concatenate(
            [rotate(kv_acc[64 * g : 64 * g + 32, :], kv_acc[64 * g + 32 : 64 * g + 64, :]) for g in range(2)], 0
        )
        kv_own[slot, 0] = keys.T.astype(BF16)

        @pl.when(x < chips - 1)
        def _():
            kv_copy(slot, 0).start()

        kv_own[slot, 1] = (kv_acc[128:256, :] * scale).astype(BF16)

        @pl.when(x < chips - 1)
        def _():
            kv_copy(slot, 1).start()

        q_acc[...] += dot(wq[kt], piece)
        for i in range(q.shape[0] // HEAD_DIM):
            first = q_acc[HEAD_DIM * i : HEAD_DIM * i + HALF, :]
            second = q_acc[HEAD_DIM * i + HALF : HEAD_DIM * (i + 1), :]
            q[HEAD_DIM * i : HEAD_DIM * (i + 1), :] = rotate(first, second).astype(BF16)

        cache_local(slot, 0).start()
        cache_remote(slot, 0, c).start()

        @pl.when(x > 0)
        def _():
            kv_copy(slot, 0).wait_recv()
            kv_copy(slot, 1).wait_recv()

        blank = jnp.zeros((HEAD_DIM, 256), BF16)
        ones = jnp.ones((16, 256), BF16)
        for p in range(shards):
            g = p // (shards // 2)
            pair = jnp.concatenate([q[128 * p : 128 * p + 64, :], q[128 * p + 64 : 128 * p + 128, :]], 1)
            pair = jnp.concatenate([pair, blank] if g == 0 else [blank, pair], 0)
            both = dot(jnp.concatenate([kv_own[slot, 0], kv_prev[slot, 0]], 0), pair)
            scores = jnp.where(lower_pair, both[:WIN], both[WIN:]) + bias
            sink = jnp.concatenate([sink_in[2 * p : 2 * p + 1, :], sink_in[2 * p + 1 : 2 * p + 2, :]], 1)
            top = jnp.maximum(jnp.max(scores, 0, keepdims=True), sink)
            expo = jnp.exp(scores - top)
            weights = jnp.concatenate(
                [jnp.where(lower_pair, expo, 0.0).astype(BF16), jnp.where(lower_pair, 0.0, expo).astype(BF16)], 0
            )
            values = jnp.concatenate(
                [kv_own[slot, 1, 64 * g : 64 * g + 64, :], kv_prev[slot, 1, 64 * g : 64 * g + 64, :]], 1
            )
            mixed = dot(jnp.concatenate([values, ones], 0), weights)
            total = mixed[HEAD_DIM : HEAD_DIM + 1, :] + jnp.exp(sink - top)
            context = (mixed[:HEAD_DIM, :] * (1.0 / total)).astype(BF16)
            base = pl.multiple_of(128 * shards * c + 128 * p, 128)
            ctx[slot, pl.ds(base, 64), :] = context[:, :128]
            ctx[slot, pl.ds(base + 64, 64), :] = context[:, 128:]
            if p % 2 == 1:
                ctx_copy(slot, c, p // 2).start()

        for k in range(tiles):
            total = jnp.zeros((TILE, 128), F32)
            for m in range(ctx_tiles):
                total = total + dot(wo[ctx_tiles * c + m, TILE * k : TILE * (k + 1), :], ctx[slot, ctx_tile(c, m), :])
            o_acc[TILE * k : TILE * (k + 1), :] = total
        for m in range(ctx_tiles):
            ctx_copy(slot, other, m).wait_recv()
        for k in range(tiles):
            total = o_acc[TILE * k : TILE * (k + 1), :]
            for m in range(ctx_tiles):
                total = total + dot(
                    wo[ctx_tiles * other + m, TILE * k : TILE * (k + 1), :], ctx[slot, ctx_tile(other, m), :]
                )
            row = pl.multiple_of(TILE * (tiles * c + k), TILE)
            h_new[slot, k] = (h[slot, pl.ds(row, TILE), :].astype(F32) + total).astype(BF16)

            @pl.when(section < sections - 1)
            def _():
                pass_on(slot, k).start()

        stage_v[slot] = kv_own[slot, 1].astype(F32).T.astype(BF16)
        cache_local(slot, 1).start()
        cache_remote(slot, 1, c).start()
        for k in range(tiles):
            stage_h[slot, k] = h_new[slot, k].astype(F32).T.astype(BF16)
            hid_local(slot, k).start()
            hid_remote(slot, k, c).start()
        return carry

    lax.fori_loop(0, micro, one_slot, 0)

    def finish(slot, carry):
        for k in range(tiles):
            hid_local(slot, k).wait()
            hid_remote(slot, k, other).wait_recv()
            hid_remote(slot, k, c).wait_send()

            @pl.when(section < sections - 1)
            def _():
                pass_on(slot, k).wait_send()

            @pl.when(section > 0)
            def _():
                forward(slot, k, c).wait_send()

        for which in range(2):
            cache_local(slot, which).wait()
            cache_remote(slot, which, other).wait_recv()
            cache_remote(slot, which, c).wait_send()

            @pl.when(x < chips - 1)
            def _():
                kv_copy(slot, which).wait_send()

        for m in range(ctx_tiles):
            ctx_copy(slot, c, m).wait_send()
        return carry

    lax.fori_loop(0, micro, finish, 0)
    each_step(settle)
    own_query(0, chip(1, home)).wait_send()
    own_query(1, chip(-1, home)).wait_send()
    for half in range(2):
        own_out(half, 0, chip(1, half)).wait_send()
        own_out(half, 1, chip(-1, half)).wait_send()

    @pl.when(c != home)
    def _():
        own_query(2, partner).wait_send()

    remote(wo_in.at[other], wo_slot(x, c), wo_own.at[other, 2], wo_recv.at[me], partner).wait_send()


def per_device(seqs, sections, tokens, block_order, prompt_lengths, norm_gain, w_query, w_key_value, w_out, sinks):
    micro, rows, width = tokens.shape
    padded = -(-width // (2 * TILE)) * 2 * TILE
    tiles = padded // (2 * TILE)
    shards = seqs // 2
    me = lax.axis_index("seq")
    core = me % 2
    extra = padded - width
    gain = norm_gain[0][:, None]
    kv_width = w_key_value.shape[2] // 2

    def turned(weight):
        weight = jnp.pad(weight.astype(BF16), ((0, extra), (0, 0)))
        return weight.reshape(padded // TILE, TILE, weight.shape[1]).transpose(0, 2, 1)

    wq = turned(w_query[0].astype(F32) * (gain * (HEAD_DIM**-0.5)))
    pair = jnp.concatenate(
        [
            lax.dynamic_slice_in_dim(w_key_value[0], core * (kv_width // 2), kv_width // 2, 1),
            lax.dynamic_slice_in_dim(w_key_value[0], kv_width + core * (kv_width // 2), kv_width // 2, 1),
        ],
        1,
    )
    wkv = turned(pair.astype(F32) * gain)
    wo = jnp.pad(w_out[0], ((0, 0), (0, extra))).reshape(w_out.shape[1], 2, padded // 2).transpose(1, 2, 0)
    tok = jnp.pad(tokens[block_order], ((0, 0), (0, 0), (0, extra)))
    lengths = prompt_lengths[block_order]
    freq = jnp.exp(jnp.arange(HALF, dtype=F32) * (-2.0 * math.log(THETA) / HEAD_DIM))
    positions = (me // 2) * (2 * rows) + jnp.arange(2 * rows, dtype=jnp.int32)
    angles = freq[:, None] * positions.astype(F32)[None, :]
    heads = 2 * shards
    sink = lax.dynamic_slice_in_dim(sinks[0], core * heads, heads, 0)
    sink = jnp.broadcast_to(sink[:, None], (heads, 128))

    vmem = pl.BlockSpec(memory_space=pltpu.VMEM)
    dma = pltpu.SemaphoreType.DMA
    cells = 64 * heads
    hidden, cache = pl.pallas_call(
        functools.partial(kernel, seqs, sections, micro, width),
        out_shape=(
            jax.ShapeDtypeStruct((micro, rows, padded), BF16),
            jax.ShapeDtypeStruct((micro, rows, 2 * kv_width), BF16),
        ),
        in_specs=[vmem] * 7 + [pl.BlockSpec(memory_space=pltpu.SMEM)],
        out_specs=(pl.BlockSpec(memory_space=pl.ANY), pl.BlockSpec(memory_space=pl.ANY)),
        scratch_shapes=[
            pltpu.VMEM((2 * tiles, cells, TILE), BF16),
            pltpu.VMEM((shards, tiles * TILE, TILE), BF16),
            pltpu.VMEM((micro, padded, 128), BF16),
            pltpu.VMEM((micro, 128, padded), BF16),
            pltpu.VMEM((256, 128), F32),
            pltpu.VMEM((cells, 128), F32),
            pltpu.VMEM((cells, 128), BF16),
            pltpu.VMEM((micro, 2, 128, 128), BF16),
            pltpu.VMEM((micro, 2, 128, 128), BF16),
            pltpu.VMEM((micro, 2 * cells, 128), BF16),
            pltpu.VMEM((tiles * TILE, 128), F32),
            pltpu.VMEM((micro, tiles, TILE, 128), BF16),
            pltpu.VMEM((micro, tiles, 128, TILE), BF16),
            pltpu.VMEM((micro, 128, 128), BF16),
            dma((shards,)), dma((3,)), dma((shards,)),
            dma((seqs,)), dma((2, 3)), dma((seqs,)),
            dma, dma((2,)),
            dma((micro, tiles)), dma((micro, tiles)),
            dma((micro, tiles)), dma((micro, tiles)),
            dma((micro, 2)), dma((micro, 2)),
            dma((micro, shards // 2)), dma((micro, shards // 2)),
            dma((micro, tiles)), dma((micro, tiles)), dma((micro, tiles)),
            dma((micro, 2)), dma((micro, 2)), dma((micro, 2)),
        ],
        compiler_params=pltpu.CompilerParams(
            collective_id=0, has_side_effects=True, vmem_limit_bytes=50 * 1024 * 1024
        ),
    )(wq, wkv, wo, tok, jnp.cos(angles), jnp.sin(angles), sink, lengths)
    return hidden[None, :, :, :width], cache[None]


def solution(mesh):
    in_specs = (
        P("groups", "seq", None),
        P("groups"),
        P("groups"),
        P("section", None),
        P("section", None, "seq"),
        P("section", None, None),
        P("section", "seq", None),
        P("section", None),
    )
    out_specs = (P("section", "groups", "seq", None), P("section", "groups", "seq", None))
    body = functools.partial(per_device, mesh.shape["seq"], mesh.shape["section"])
    return jax.shard_map(body, mesh=mesh, in_specs=in_specs, out_specs=out_specs, check_vma=False)
```

time: 788 us -> 318 us (0.40)
  the two profiles are of different devices: /device:TPU:1858 before, /device:TPU:1999 now
where the time goes in v1:
time: 318 us; the launch traced here: 317 us
  Pallas kernels  308 us (97%)
  local copies, waits for them, and re-layouts  5.19 us (2%)
    pallas_call x1, Pallas kernels, per_device(): pl.pallas_call(functools.partial(kernel, seqs, sections, micro, width), o...  308 us

profile of v1, /device:TPU:1999, one launch (start us, length us, event | category | flops | bytes accessed | tf_op | source)
XLA Modules:
  0.0 317.4 jit_solution(5923208415975059207)
XLA Ops:
  0.6 0.0 copy-start
  0.7 0.0 copy-start.2
  0.7 0.8 fusion.1
  1.5 0.7 compare_select_fusion
  2.2 1.3 gather_fusion.1
  3.5 0.1 broadcast_in_dim.22.sink_in
  3.6 0.7 reduce
  4.3 0.1 multiply_sine_fusion
  4.4 0.0 copy-start.1
  4.4 1.4 fusion
  5.8 0.2 copy.10
  6.0 0.0 copy-done.2
  6.1 0.0 copy-done.1
  6.1 0.1 dynamic-slice_bitcast_fusion.1
  6.2 0.3 multiply_convert_fusion
  6.5 0.1 pad.17
  6.5 0.3 copy.11
  6.8 0.0 copy-done
  6.8 0.6 gather_fusion
  7.4 0.1 pad.19.tok_in
  7.5 308.3 %shard_map.95 = (bf16[4,64,1536]{2,1,0:T(8,128)(2,1)S(1)}, bf16[4,64,512]{2,1,0:T(8,128)(2,1)S(1)}) custom-call(bf16[6,128,256]{2,1,0:T(8,128)(2,1)S(1)} %bitcast.21, bf16[6,256,256]{2,1,0:T(8,128)(2,1)S(1)} %bitcast.20, bf16[2,768,128]{2,1,0:T(8,128)(2,1)S(1)} %bitcast.22, bf16[4,64,1536]{2,1,0:T(8,128)(2,1)S(1)} %pad.19.tok_in, ...), custom_call_target="tpu_custom_call" | custom-call | tf_op jit(solution)/shard_map/pallas_call | solution.py:447
  315.8 0.9 slice_bitcast_fusion
  316.7 0.7 copy.13
  (6 shorter events, 0.1 us)
Async XLA Ops:
  0.6 6.2 %copy-start = (bf16[4,64,1440]{2,1,0:T(8,128)(2,1)S(1)}, bf16[4,64,1440]{2,1,0:T(8,128)(2,1)}, u32[]{:S(2)}) copy-start(bf16[4,64,1440]{2,1,0:T(8,128)(2,1)} %param.8) | copy-start | bytes 2211844
  0.7 5.4 %copy-start.2 = (bf16[1,128,1440]{1,2,0:T(8,128)(2,1)S(1)}, bf16[1,128,1440]{1,2,0:T(8,128)(2,1)}, u32[]{:S(2)}) copy-start(bf16[1,128,1440]{1,2,0:T(8,128)(2,1)} %param.14) | copy-start | bytes 1105924
  4.4 1.7 copy-start.1

commit v2 on v1

--- a/solution.py
+++ b/solution.py
@@ -16,6 +16,7 @@
 THETA = 150000.0
 EPSILON = 1e-05
 LOW = -1e30
+LOG2E = math.log2(math.e)
 F32 = jnp.float32
 BF16 = jnp.bfloat16
 
@@ -168,12 +169,15 @@
 
         lax.fori_loop(0, micro, turn, 0)
 
+    @pl.when(section > 0)
+    def _():
+        h[:, width:, :] = jnp.zeros((micro, h.shape[1] - width, 128), BF16)
+
     @pl.when(x == 0)
     def _():
         kv_prev[...] = jnp.zeros_like(kv_prev)
 
     each_step(relay)
-    own_slot = wq_slot(2 * (x % half_chips))
 
     @pl.when(c == home)
     def _():
@@ -184,14 +188,31 @@
     for core in range(2):
         pltpu.make_async_copy(wo_in.at[0], wo_slot(x, core), wo_recv.at[2 * x + core]).wait()
 
-    def h_tile(slot, k):
-        return h.at[slot, pl.ds(pl.multiple_of(TILE * k, TILE), TILE), :]
-
-    def pass_on(slot, k):
-        return remote(h_new.at[slot, k], h_tile(slot, tiles * c + k), h_send.at[slot, k], h_recv.at[slot, k], up)
-
-    def forward(slot, k, core):
-        piece = h_tile(slot, tiles * core + k)
+    short = width - (2 * tiles - 1) * TILE
+
+    def sized(core, k, act):
+        if k < tiles - 1 or short == TILE:
+            act(TILE)
+        else:
+
+            @pl.when(core == 0)
+            def _():
+                act(TILE)
+
+            @pl.when(core == 1)
+            def _():
+                act(short)
+
+    def h_tile(slot, k, size):
+        return h.at[slot, pl.ds(pl.multiple_of(TILE * k, TILE), size), :]
+
+    def pass_on(slot, k, size):
+        return remote(
+            h_new.at[slot, k, :size, :], h_tile(slot, tiles * c + k, size), h_send.at[slot, k], h_recv.at[slot, k], up
+        )
+
+    def forward(slot, k, core, size):
+        piece = h_tile(slot, tiles * core + k, size)
         return remote(piece, piece, f_send.at[slot, k], f_recv.at[slot, k], partner)
 
     def kv_copy(slot, which):
@@ -260,11 +281,14 @@
 
                 @pl.when(section > 0)
                 def _():
-                    if own:
-                        pass_on(slot, k).wait_recv()
-                        forward(slot, k, c).start()
-                    else:
-                        forward(slot, k, other).wait_recv()
+                    def arrive(size):
+                        if own:
+                            pass_on(slot, k, size).wait_recv()
+                            forward(slot, k, c, size).start()
+                        else:
+                            forward(slot, k, other, size).wait_recv()
+
+                    sized(core, k, arrive)
 
                 piece = h[slot, pl.ds(pl.multiple_of(TILE * kt, TILE), TILE), :]
                 wide = piece.astype(F32)
@@ -310,29 +334,39 @@
 
         blank = jnp.zeros((HEAD_DIM, 256), BF16)
         ones = jnp.ones((16, 256), BF16)
-        for p in range(shards):
-            g = p // (shards // 2)
+        own_mask = lower_pair.astype(F32).astype(BF16)
+        prev_mask = 1 - own_mask
+        all_keys = jnp.concatenate([kv_own[slot, 0], kv_prev[slot, 0]], 0)
+        group = shards // 2
+
+        def raw_scores(p):
             pair = jnp.concatenate([q[128 * p : 128 * p + 64, :], q[128 * p + 64 : 128 * p + 128, :]], 1)
-            pair = jnp.concatenate([pair, blank] if g == 0 else [blank, pair], 0)
-            both = dot(jnp.concatenate([kv_own[slot, 0], kv_prev[slot, 0]], 0), pair)
-            scores = jnp.where(lower_pair, both[:WIN], both[WIN:]) + bias
-            sink = jnp.concatenate([sink_in[2 * p : 2 * p + 1, :], sink_in[2 * p + 1 : 2 * p + 2, :]], 1)
-            top = jnp.maximum(jnp.max(scores, 0, keepdims=True), sink)
-            expo = jnp.exp(scores - top)
-            weights = jnp.concatenate(
-                [jnp.where(lower_pair, expo, 0.0).astype(BF16), jnp.where(lower_pair, 0.0, expo).astype(BF16)], 0
-            )
+            return dot(all_keys, jnp.concatenate([pair, blank] if p < group else [blank, pair], 0))
+
+        for g in range(2):
+            pairs = range(group * g, group * (g + 1))
+            raw = [raw_scores(p) for p in pairs]
             values = jnp.concatenate(
                 [kv_own[slot, 1, 64 * g : 64 * g + 64, :], kv_prev[slot, 1, 64 * g : 64 * g + 64, :]], 1
             )
-            mixed = dot(jnp.concatenate([values, ones], 0), weights)
-            total = mixed[HEAD_DIM : HEAD_DIM + 1, :] + jnp.exp(sink - top)
-            context = (mixed[:HEAD_DIM, :] * (1.0 / total)).astype(BF16)
-            base = pl.multiple_of(128 * shards * c + 128 * p, 128)
-            ctx[slot, pl.ds(base, 64), :] = context[:, :128]
-            ctx[slot, pl.ds(base + 64, 64), :] = context[:, 128:]
-            if p % 2 == 1:
-                ctx_copy(slot, c, p // 2).start()
+            values = jnp.concatenate([values, ones], 0)
+            mixed = []
+            rests = []
+            for p, both in zip(pairs, raw):
+                scores = jnp.where(lower_pair, both[:WIN], both[WIN:]) + bias
+                sink = jnp.concatenate([sink_in[2 * p : 2 * p + 1, :], sink_in[2 * p + 1 : 2 * p + 2, :]], 1)
+                top = jnp.maximum(jnp.max(scores, 0, keepdims=True), sink)
+                expo = jnp.exp2(scores - top).astype(BF16)
+                mixed.append(dot(values, jnp.concatenate([expo * own_mask, expo * prev_mask], 0)))
+                rests.append(jnp.exp2(sink - top))
+            for p, mix, rest in zip(pairs, mixed, rests):
+                total = mix[HEAD_DIM : HEAD_DIM + 1, :] + rest
+                context = (mix[:HEAD_DIM, :] * (1.0 / total)).astype(BF16)
+                base = pl.multiple_of(128 * shards * c + 128 * p, 128)
+                ctx[slot, pl.ds(base, 64), :] = context[:, :128]
+                ctx[slot, pl.ds(base + 64, 64), :] = context[:, 128:]
+            for m in range(group * g // 2, group * (g + 1) // 2):
+                ctx_copy(slot, c, m).start()
 
         for k in range(tiles):
             total = jnp.zeros((TILE, 128), F32)
@@ -352,7 +386,7 @@
 
             @pl.when(section < sections - 1)
             def _():
-                pass_on(slot, k).start()
+                sized(c, k, lambda size: pass_on(slot, k, size).start())
 
         stage_v[slot] = kv_own[slot, 1].astype(F32).T.astype(BF16)
         cache_local(slot, 1).start()
@@ -373,11 +407,11 @@
 
             @pl.when(section < sections - 1)
             def _():
-                pass_on(slot, k).wait_send()
+                sized(c, k, lambda size: pass_on(slot, k, size).wait_send())
 
             @pl.when(section > 0)
             def _():
-                forward(slot, k, c).wait_send()
+                sized(c, k, lambda size: forward(slot, k, c, size).wait_send())
 
         for which in range(2):
             cache_local(slot, which).wait()
@@ -422,7 +456,7 @@
         weight = jnp.pad(weight.astype(BF16), ((0, extra), (0, 0)))
         return weight.reshape(padded // TILE, TILE, weight.shape[1]).transpose(0, 2, 1)
 
-    wq = turned(w_query[0].astype(F32) * (gain * (HEAD_DIM**-0.5)))
+    wq = turned(w_query[0].astype(F32) * (gain * (HEAD_DIM**-0.5 * LOG2E)))
     pair = jnp.concatenate(
         [
             lax.dynamic_slice_in_dim(w_key_value[0], core * (kv_width // 2), kv_width // 2, 1),
@@ -439,7 +473,7 @@
     angles = freq[:, None] * positions.astype(F32)[None, :]
     heads = 2 * shards
     sink = lax.dynamic_slice_in_dim(sinks[0], core * heads, heads, 0)
-    sink = jnp.broadcast_to(sink[:, None], (heads, 128))
+    sink = jnp.broadcast_to(sink[:, None] * LOG2E, (heads, 128))
 
     vmem = pl.BlockSpec(memory_space=pltpu.VMEM)
     dma = pltpu.SemaphoreType.DMA

time: 318 us -> 293 us (0.921)
  Pallas kernels: 308 us -> 283 us
    pallas_call x1, Pallas kernels: 308 us -> 283 us  [per_device(): pl.pallas_call(functools.partial(kernel, seqs, sections, micro, width), o...]
where the time goes in v2:
time: 293 us; the launch traced here: 292 us
  Pallas kernels  283 us (97%)
  local copies, waits for them, and re-layouts  4.37 us (1%)
  other arithmetic  3.98 us (1%)
    pallas_call x1, Pallas kernels, per_device(): pl.pallas_call(functools.partial(kernel, seqs, sections, micro, width), o...  283 us

profile of v2, /device:TPU:1999, one launch (start us, length us, event | category | flops | bytes accessed | tf_op | source)
XLA Modules:
  0.0 292.3 jit_solution(4315812873668966713)
XLA Ops:
  0.6 0.0 copy-start
  0.7 0.0 copy-start.2
  0.7 0.8 fusion.2
  1.5 0.7 compare_select_fusion
  2.2 1.3 gather_fusion.1
  3.5 0.1 broadcast_in_dim.9.sink_in
  3.6 0.7 reduce
  4.3 0.1 multiply_sine_fusion
  4.4 0.0 copy-start.1
  4.5 1.4 fusion
  5.8 0.2 copy.10
  6.0 0.0 copy-done.2
  6.1 0.0 copy-done.1
  6.1 0.1 dynamic-slice_bitcast_fusion.1
  6.2 0.3 multiply_convert_fusion
  6.5 0.1 pad.17
  6.5 0.3 copy.11
  6.8 0.0 copy-done
  6.8 0.6 gather_fusion
  7.4 0.1 pad.19.tok_in
  7.5 283.2 %shard_map.95 = (bf16[4,64,1536]{2,1,0:T(8,128)(2,1)S(1)}, bf16[4,64,512]{2,1,0:T(8,128)(2,1)S(1)}) custom-call(bf16[6,128,256]{2,1,0:T(8,128)(2,1)S(1)} %bitcast.21, bf16[6,256,256]{2,1,0:T(8,128)(2,1)S(1)} %bitcast.20, bf16[2,768,128]{2,1,0:T(8,128)(2,1)S(1)} %bitcast.22, bf16[4,64,1536]{2,1,0:T(8,128)(2,1)S(1)} %pad.19.tok_in, ...), custom_call_target="tpu_custom_call" | custom-call | tf_op jit(solution)/shard_map/pallas_call | solution.py:481
  290.7 0.9 slice_bitcast_fusion
  291.6 0.7 copy.13
  (6 shorter events, 0.1 us)
Async XLA Ops:
  0.6 6.2 %copy-start = (bf16[4,64,1440]{2,1,0:T(8,128)(2,1)S(1)}, bf16[4,64,1440]{2,1,0:T(8,128)(2,1)}, u32[]{:S(2)}) copy-start(bf16[4,64,1440]{2,1,0:T(8,128)(2,1)} %param.8) | copy-start | bytes 2211844
  0.7 5.4 %copy-start.2 = (bf16[1,128,1440]{1,2,0:T(8,128)(2,1)S(1)}, bf16[1,128,1440]{1,2,0:T(8,128)(2,1)}, u32[]{:S(2)}) copy-start(bf16[1,128,1440]{1,2,0:T(8,128)(2,1)} %param.14) | copy-start | bytes 1105924
  4.4 1.7 copy-start.1

commit v3 on v2

--- a/solution.py
+++ b/solution.py
@@ -27,10 +27,11 @@
 
 def kernel(
     seqs, sections, micro, width,
-    wq_in, wkv_in, wo_in, tok_in, cos_in, sin_in, sink_in, length_in,
+    wq_in, wkv_in, wo_in, tok_in, cos_in, sin_in, sink_in, length_in, order_in,
     hid_out, cache_out,
-    wq, wo, h, tok, kv_acc, q_acc, q, kv_own, kv_prev, ctx, o_acc, h_new, stage_h, stage_v,
+    wq, wo, h, tok, kv_acc, q_acc, q, kv_own, kv_prev, ctx, o_acc, h_new, stage_h, stage_v, aq, ao,
     wq_recv, wq_own, wq_relay, wo_recv, wo_own, wo_relay,
+    aq_recv, aq_relay, aq_up, ao_recv, ao_relay, ao_up,
     tok_send, tok_recv, h_send, h_recv, f_send, f_recv, kv_send, kv_recv, c_send, c_recv,
     oh_local, oh_send, oh_recv, oc_local, oc_send, oc_recv,
 ):
@@ -38,6 +39,7 @@
     half_chips = chips // 2
     shards = seqs // 2
     tiles = h.shape[1] // (2 * TILE)
+    cut = TILE * tiles - ao.shape[1]
     ctx_tiles = shards // 2
     me = lax.axis_index("seq")
     section = lax.axis_index("section")
@@ -54,96 +56,297 @@
             src_ref=src, dst_ref=dst, send_sem=send, recv_sem=recv, device_id=target, device_id_type=MESH
         )
 
-    up = {"section": (section + 1) % sections}
-    down = {"section": (section + sections - 1) % sections}
+    first = section == 0
+    last = section == sections - 1
+    above = (section + 1) % sections
+    below = (section + sections - 1) % sections
+    up = {"section": above}
     barrier = pltpu.get_barrier_semaphore()
-    for target in (partner, chip(1, 0), chip(1, 1), chip(-1, 0), chip(-1, 1), up, down):
+    greeted = [partner] + [chip(step, core) for step in (1, -1) for core in range(2)]
+    greeted += [{"section": level, "seq": 2 * x + core} for level in (above, below) for core in range(2)]
+    for target in greeted:
         pl.semaphore_signal(barrier, inc=1, device_id=target, device_id_type=MESH)
-    pl.semaphore_wait(barrier, 7)
+    pl.semaphore_wait(barrier, len(greeted))
 
     home = x // half_chips
-
-    def wq_slot(index):
-        return wq.at[:, pl.ds(pl.multiple_of(128 * index, 128), 128), :]
-
-    def wo_slot(owner, core):
-        return wo.at[owner, :, pl.ds(pl.multiple_of(128 * core, 128), 128)]
+    query_cuts = (0, tiles, 2 * tiles - 1, 2 * tiles)
+    out_cuts = (0, cut, TILE * tiles)
+    dead = h.shape[1] - width
+    query_pieces, out_pieces = range(3), range(2)
+    query_tail, out_tail = 2, 1
+
+    def query_slot(index, piece):
+        lo, hi = query_cuts[piece : piece + 2]
+        return wq.at[lo:hi, pl.ds(pl.multiple_of(128 * index, 128), 128), :]
+
+    def out_slot(owner, core, piece):
+        lo, hi = out_cuts[piece : piece + 2]
+        return wo.at[owner, lo:hi, pl.ds(pl.multiple_of(128 * core, 128), 128)]
+
+    def query_source(piece):
+        return wq_in.at[query_cuts[piece] : query_cuts[piece + 1]]
+
+    def out_source(half, piece):
+        return wo_in.at[half, out_cuts[piece] : out_cuts[piece + 1], :]
+
+    def aid_query(index):
+        return aq.at[:, pl.ds(pl.multiple_of(128 * index, 128), 128), :]
+
+    def aid_out(owner, core, size):
+        return ao.at[owner, :size, pl.ds(pl.multiple_of(128 * core, 128), 128)]
+
+    def halves(half, act):
+        if isinstance(half, int):
+            act(TILE * tiles - cut - (dead if half else 0))
+        else:
+            for each in range(2):
+
+                @pl.when(half == each)
+                def _():
+                    act(TILE * tiles - cut - (dead if each else 0))
 
     mine = me - shards * home
 
-    def own_query(which, target):
-        return remote(wq_in, wq_slot(mine), wq_own.at[which], wq_recv.at[mine], target)
-
-    def local_query():
-        return pltpu.make_async_copy(wq_in, wq_slot(mine), wq_recv.at[mine])
-
-    def own_out(half, which, target):
-        return remote(wo_in.at[half], wo_slot(x, c), wo_own.at[half, which], wo_recv.at[me], target)
-
-    def local_out():
-        return pltpu.make_async_copy(wo_in.at[c], wo_slot(x, c), wo_recv.at[me])
-
-    own_query(0, chip(1, home)).start()
-    own_query(1, chip(-1, home)).start()
-    for half in range(2):
-        own_out(half, 0, chip(1, half)).start()
-        own_out(half, 1, chip(-1, half)).start()
-
-    @pl.when(c == home)
-    def _():
-        local_query().start()
-
-    @pl.when(c != home)
-    def _():
-        own_query(2, partner).start()
-
-    local_out().start()
-    remote(wo_in.at[other], wo_slot(x, c), wo_own.at[other, 2], wo_recv.at[me], partner).start()
-
-    def query_copy(index, sign):
-        return remote(wq_slot(index), wq_slot(index), wq_relay.at[index], wq_recv.at[index], chip(sign, c))
-
-    def out_copy(owner, core, sign):
-        slot = wo_slot(owner, core)
-        return remote(slot, slot, wo_relay.at[2 * owner + core], wo_recv.at[2 * owner + core], chip(sign, c))
-
-    def each_query(step, sign, hops, act):
-        owner = (x - sign * step + chips) % chips
-
-        @pl.when((step <= hops) & (owner // half_chips == c))
+    def own_query(piece, which, target):
+        return remote(
+            query_source(piece), query_slot(mine, piece), wq_own.at[piece, which], wq_recv.at[piece, mine], target
+        )
+
+    def local_query(piece, index):
+        return pltpu.make_async_copy(query_source(piece), query_slot(index, piece), wq_recv.at[piece, index])
+
+    def own_out(half, piece, which, target):
+        return remote(
+            out_source(half, piece), out_slot(x, c, piece), wo_own.at[half, piece, which], wo_recv.at[piece, me], target
+        )
+
+    def local_out(piece, core):
+        return pltpu.make_async_copy(out_source(c, piece), out_slot(x, core, piece), wo_recv.at[piece, 2 * x + core])
+
+    def lend_query():
+        target = {"section": below, "seq": 2 * x + home}
+        return remote(query_source(query_tail), aid_query(mine), wq_own.at[query_tail, 0], aq_recv.at[mine], target)
+
+    def lend_out(half, size):
+        target = {"section": below, "seq": 2 * x + half}
+        source = wo_in.at[half, cut : cut + size, :]
+        return remote(source, aid_out(x, c, size), wo_own.at[half, out_tail, 0], ao_recv.at[me], target)
+
+    def own_queries(act):
+        for piece in query_pieces:
+
+            def ring():
+                act(own_query(piece, 0, chip(1, home)))
+                act(own_query(piece, 1, chip(-1, home)))
+
+            if piece == query_tail:
+                pl.when(~first)(ring)
+                pl.when(first)(lambda: act(lend_query()))
+            else:
+                ring()
+
+            @pl.when(c != home)
+            def _():
+                act(own_query(piece, 2, partner))
+
+    def own_outs(act):
+        for piece in out_pieces:
+            for half in range(2):
+
+                def ring():
+                    act(own_out(half, piece, 0, chip(1, half)))
+                    act(own_out(half, piece, 1, chip(-1, half)))
+
+                if piece == out_tail:
+                    pl.when(~first)(ring)
+                else:
+                    ring()
+            act(own_out(other, piece, 2, partner))
+
+    def lend_outs(act):
+        @pl.when(first)
+        def _():
+            for half in range(2):
+                halves(half, lambda size: act(lend_out(half, size)))
+
+    def query_copy(index, sign, piece):
+        slot = query_slot(index, piece)
+        return remote(slot, slot, wq_relay.at[piece, index], wq_recv.at[piece, index], chip(sign, c))
+
+    def out_copy(owner, core, sign, piece):
+        slot = out_slot(owner, core, piece)
+        index = 2 * owner + core
+        return remote(slot, slot, wo_relay.at[piece, index], wo_recv.at[piece, index], chip(sign, c))
+
+    def owner_of(step, sign):
+        return (x - sign * step + chips) % chips
+
+    query_hops = {1: half_chips, -1: half_chips - 1}
+    out_hops = {1: half_chips - 1, -1: half_chips}
+
+    def each_query(step, sign, act):
+        owner = owner_of(step, sign)
+        held = owner // half_chips == c
+        for piece in query_pieces:
+
+            @pl.when(held & ~first if piece == query_tail else held)
+            def _():
+                for core in range(2):
+                    index = 2 * owner + core - shards * c
+                    act(lambda: query_copy(index, sign, piece), step < query_hops[sign])
+
+    def each_out(step, sign, act):
+        owner = owner_of(step, sign)
+        for piece in out_pieces:
+
+            def held():
+                for core in range(2):
+                    act(lambda: out_copy(owner, core, sign, piece), step < out_hops[sign])
+
+            if piece == out_tail:
+                pl.when(~first)(held)
+            else:
+                held()
+
+    arrivals = []
+    for sign in (1, -1):
+        line = [(each_query, step) for step in range(1, half_chips)] + [(each_out, 1)]
+        line += [(each_query, step) for step in range(half_chips, query_hops[sign] + 1)]
+        line += [(each_out, step) for step in range(2, out_hops[sign] + 1)]
+        time = 0
+        for kind, step in line:
+            time += 5 if kind is each_query else 3
+            arrivals.append((time, sign, kind, step))
+    arrivals.sort(key=lambda arrival: (arrival[0], -arrival[1]))
+    needed = [a for a in range(len(arrivals)) if arrivals[a][2] is each_query][-1] + 1
+    ending = max(needed, len(arrivals) - 2)
+
+    def take(low, high, act):
+        for _, sign, kind, step in arrivals[low:high]:
+            kind(step, sign, act)
+
+    def relay(make, more):
+        copy = make()
+        copy.wait_recv()
+        if more:
+            copy.start()
+
+    def settle(make, more):
+        if more:
+            make().wait_send()
+
+    def steps(low, high, each, act):
+        def body(step, carry):
+            each(step, act)
+            return carry
+
+        lax.fori_loop(low, high, body, 0)
+
+    def aid_query_copy(index, sign):
+        slot = aid_query(index)
+        return remote(slot, slot, aq_relay.at[(1 - sign) // 2, index], aq_recv.at[index], chip(sign, c))
+
+    def aid_query_up(index):
+        return remote(
+            aid_query(index), query_slot(index, query_tail), aq_up.at[index], wq_recv.at[query_tail, index], up
+        )
+
+    def aid_out_copy(owner, core, sign, size):
+        slot = aid_out(owner, core, size)
+        index = 2 * owner + core
+        return remote(slot, slot, ao_relay.at[(1 - sign) // 2, index], ao_recv.at[index], chip(sign, c))
+
+    def aid_out_up(owner, core, size):
+        index = 2 * owner + core
+        target = wo.at[owner, cut : cut + size, pl.ds(pl.multiple_of(128 * core, 128), 128)]
+        return remote(aid_out(owner, core, size), target, ao_up.at[index], wo_recv.at[out_tail, index], up)
+
+    def aid_own_query(act):
+        @pl.when(c == home)
         def _():
             for core in range(2):
-                act(query_copy(2 * owner + core - shards * c, sign), step < hops)
-
-    def each_out(step, sign, hops, act):
-        owner = (x - sign * step + chips) % chips
-
-        @pl.when(step <= hops)
-        def _():
+                index = 2 * x + core - shards * c
+                act(aid_query_copy(index, 1), aid_query_copy(index, -1))
+
+    def aid_own_out(act):
+        def both(size):
             for core in range(2):
-                act(out_copy(owner, core, sign), step < hops)
-
-    def relay(copy, more):
-        copy.wait_recv()
+                act(aid_out_copy(x, core, 1, size), aid_out_copy(x, core, -1, size))
+
+        halves(c, both)
+
+    def aid_each_query(step, act):
+        for sign in (1, -1):
+            owner = owner_of(step, sign)
+
+            @pl.when((step <= query_hops[sign]) & (owner // half_chips == c))
+            def _():
+                for core in range(2):
+                    index = 2 * owner + core - shards * c
+                    act(aid_query_copy(index, sign), aid_query_up(index), step < query_hops[sign])
+
+    def aid_each_out(step, act):
+        for sign in (-1, 1):
+            owner = owner_of(step, sign)
+
+            @pl.when(step <= out_hops[sign])
+            def _():
+                def both(size):
+                    for core in range(2):
+                        act(
+                            aid_out_copy(owner, core, sign, size), aid_out_up(owner, core, size),
+                            step < out_hops[sign],
+                        )
+
+                halves(c, both)
+
+    def aid_send(right, left):
+        right.wait_recv()
+        right.start()
+        left.start()
+
+    def aid_sent(right, left):
+        right.wait_send()
+        left.wait_send()
+
+    def aid_relay(along, upward, more):
+        along.wait_recv()
+        upward.start()
 
         @pl.when(more)
         def _():
-            copy.start()
-
-    def settle(copy, more):
+            along.start()
+
+    def aid_settle(along, upward, more):
+        upward.wait_send()
+
         @pl.when(more)
         def _():
-            copy.wait_send()
-
-    def each_step(act):
-        def body(step, carry):
-            each_query(step, 1, half_chips, act)
-            each_query(step, -1, half_chips - 1, act)
-            each_out(step, -1, half_chips, act)
-            each_out(step, 1, half_chips - 1, act)
-            return carry
-
-        lax.fori_loop(1, half_chips + 1, body, 0)
+            along.wait_send()
+
+    def start(copy):
+        copy.start()
+
+    def sent(copy):
+        copy.wait_send()
+
+    @pl.when(last)
+    def _():
+        aid_own_query(aid_send)
+        aid_own_out(aid_send)
+        steps(1, half_chips + 1, aid_each_query, aid_relay)
+        steps(1, half_chips + 1, aid_each_out, aid_relay)
+
+    own_queries(start)
+    lend_outs(start)
+    for piece in query_pieces:
+
+        @pl.when(c == home)
+        def _():
+            local_query(piece, mine).start()
+
+    for piece in out_pieces:
+        local_out(piece, c).start()
 
     rows = pl.ds(pl.multiple_of(64 * c, 64), 64)
     other_rows = pl.ds(pl.multiple_of(64 * other, 64), 64)
@@ -154,7 +357,18 @@
     def tok_local():
         return pltpu.make_async_copy(tok_in, tok.at[:, rows, :], tok_recv.at[0])
 
-    @pl.when(section == 0)
+    h[:, width:, :] = jnp.zeros((micro, h.shape[1] - width, 128), BF16)
+
+    @pl.when(first & (c == 1))
+    def _():
+        for step in range(1, chips):
+            wo[(x + step) % chips, TILE * tiles - dead :, :] = jnp.zeros((dead, TILE), BF16)
+
+    @pl.when(x == 0)
+    def _():
+        kv_prev[...] = jnp.zeros_like(kv_prev)
+
+    @pl.when(first)
     def _():
         tok_remote().start()
         tok_local().start()
@@ -162,31 +376,62 @@
         tok_remote().wait()
 
         def turn(slot, carry):
-            for k in range(2 * tiles):
-                piece = tok[slot, :, TILE * k : TILE * (k + 1)].astype(F32)
-                h[slot, TILE * k : TILE * (k + 1), :] = piece.T.astype(BF16)
+            block = order_in[slot]
+            for low in range(0, width, 128):
+                high = min(low + 128, width)
+                h[slot, low:high, :] = tok[block, :, low:high].astype(F32).T.astype(BF16)
             return carry
 
         lax.fori_loop(0, micro, turn, 0)
 
-    @pl.when(section > 0)
-    def _():
-        h[:, width:, :] = jnp.zeros((micro, h.shape[1] - width, 128), BF16)
-
-    @pl.when(x == 0)
-    def _():
-        kv_prev[...] = jnp.zeros_like(kv_prev)
-
-    each_step(relay)
+    before = 2 * (half_chips - 2)
+    take(0, before, relay)
+    own_outs(start)
+    take(before, needed, relay)
 
     @pl.when(c == home)
     def _():
-        for core in range(2):
-            index = 2 * x + core - shards * c
-            pltpu.make_async_copy(wq_in, wq_slot(index), wq_recv.at[index]).wait()
-
-    for core in range(2):
-        pltpu.make_async_copy(wo_in.at[0], wo_slot(x, core), wo_recv.at[2 * x + core]).wait()
+        for piece in query_pieces:
+            for core in range(2):
+                local_query(piece, 2 * x + core - shards * c).wait()
+
+    @pl.when(first)
+    def _():
+        def body(step, carry):
+            for sign in (1, -1):
+                owner = owner_of(step, sign)
+
+                @pl.when((step <= query_hops[sign]) & (owner // half_chips == c))
+                def _():
+                    for core in range(2):
+                        query_copy(2 * owner + core - shards * c, sign, query_tail).wait_recv()
+
+            return carry
+
+        lax.fori_loop(1, half_chips + 1, body, 0)
+
+    def finish_outs():
+        for piece in out_pieces:
+            for core in range(2):
+                local_out(piece, core).wait()
+
+        @pl.when(first)
+        def _():
+            def body(step, carry):
+                for sign in (-1, 1):
+                    owner = owner_of(step, sign)
+
+                    @pl.when(step <= out_hops[sign])
+                    def _():
+                        def both(size):
+                            for core in range(2):
+                                aid_out_up(owner, core, size).wait_recv()
+
+                        halves(c, both)
+
+                return carry
+
+            lax.fori_loop(1, half_chips + 1, body, 0)
 
     short = width - (2 * tiles - 1) * TILE
 
@@ -264,18 +509,12 @@
     lower = key <= token
     lower_pair = jnp.concatenate([lower.astype(jnp.int32)] * 2, 1) == 1
 
-    def one_slot(slot, carry):
-        length = length_in[slot]
-        allowed_own = (WIN * x + key < length) | (key == token)
-        allowed_prev = (WIN * x - WIN + key < length) & (x > 0)
-        bias = jnp.where(lower, jnp.where(allowed_own, 0.0, LOW), jnp.where(allowed_prev, 0.0, LOW))
-        bias = jnp.concatenate([bias, bias], 1)
-
+    def project(slot):
         kv_acc[...] = jnp.zeros_like(kv_acc)
         q_acc[...] = jnp.zeros_like(q_acc)
         squares = jnp.zeros((8, 128), F32)
-        for k in range(tiles):
-            for own in (True, False):
+        for own in (True, False):
+            for k in range(tiles):
                 core = c if own else other
                 kt = tiles * core + k
 
@@ -324,8 +563,12 @@
             second = q_acc[HEAD_DIM * i + HALF : HEAD_DIM * (i + 1), :]
             q[HEAD_DIM * i : HEAD_DIM * (i + 1), :] = rotate(first, second).astype(BF16)
 
-        cache_local(slot, 0).start()
-        cache_remote(slot, 0, c).start()
+    def attend(slot):
+        length = length_in[order_in[slot]]
+        allowed_own = (WIN * x + key < length) | (key == token)
+        allowed_prev = (WIN * x - WIN + key < length) & (x > 0)
+        bias = jnp.where(lower, jnp.where(allowed_own, 0.0, LOW), jnp.where(allowed_prev, 0.0, LOW))
+        bias = jnp.concatenate([bias, bias], 1)
 
         @pl.when(x > 0)
         def _():
@@ -368,19 +611,26 @@
             for m in range(group * g // 2, group * (g + 1) // 2):
                 ctx_copy(slot, c, m).start()
 
+    def emit(slot):
+        def part(core, k, m):
+            return dot(wo[ctx_tiles * core + m, TILE * k : TILE * (k + 1), :], ctx[slot, ctx_tile(core, m), :])
+
+        early, late = range(ctx_tiles // 2), range(ctx_tiles // 2, ctx_tiles)
+        for m in early:
+            ctx_copy(slot, other, m).wait_recv()
         for k in range(tiles):
-            total = jnp.zeros((TILE, 128), F32)
-            for m in range(ctx_tiles):
-                total = total + dot(wo[ctx_tiles * c + m, TILE * k : TILE * (k + 1), :], ctx[slot, ctx_tile(c, m), :])
+            total = part(c, k, 0)
+            for m in range(1, ctx_tiles):
+                total = total + part(c, k, m)
+            for m in early:
+                total = total + part(other, k, m)
             o_acc[TILE * k : TILE * (k + 1), :] = total
-        for m in range(ctx_tiles):
+        for m in late:
             ctx_copy(slot, other, m).wait_recv()
         for k in range(tiles):
             total = o_acc[TILE * k : TILE * (k + 1), :]
-            for m in range(ctx_tiles):
-                total = total + dot(
-                    wo[ctx_tiles * other + m, TILE * k : TILE * (k + 1), :], ctx[slot, ctx_tile(other, m), :]
-                )
+            for m in late:
+                total = total + part(other, k, m)
             row = pl.multiple_of(TILE * (tiles * c + k), TILE)
             h_new[slot, k] = (h[slot, pl.ds(row, TILE), :].astype(F32) + total).astype(BF16)
 
@@ -388,6 +638,8 @@
             def _():
                 sized(c, k, lambda size: pass_on(slot, k, size).start())
 
+        cache_local(slot, 0).start()
+        cache_remote(slot, 0, c).start()
         stage_v[slot] = kv_own[slot, 1].astype(F32).T.astype(BF16)
         cache_local(slot, 1).start()
         cache_remote(slot, 1, c).start()
@@ -395,6 +647,41 @@
             stage_h[slot, k] = h_new[slot, k].astype(F32).T.astype(BF16)
             hid_local(slot, k).start()
             hid_remote(slot, k, c).start()
+
+    @pl.when(first)
+    def _():
+        project(0)
+
+    take(needed, ending, relay)
+
+    @pl.when(~first)
+    def _():
+        project(0)
+
+    attend(0)
+
+    @pl.when(first)
+    def _():
+        project(1)
+
+    take(ending, len(arrivals), relay)
+    finish_outs()
+
+    def one_slot(slot, carry):
+        emit(slot)
+
+        @pl.when(~first & (slot < micro - 1))
+        def _():
+            project(slot + 1)
+
+        @pl.when(slot < micro - 1)
+        def _():
+            attend(slot + 1)
+
+        @pl.when(first & (slot < micro - 2))
+        def _():
+            project(slot + 2)
+
         return carry
 
     lax.fori_loop(0, micro, one_slot, 0)
@@ -427,18 +714,17 @@
         return carry
 
     lax.fori_loop(0, micro, finish, 0)
-    each_step(settle)
-    own_query(0, chip(1, home)).wait_send()
-    own_query(1, chip(-1, home)).wait_send()
-    for half in range(2):
-        own_out(half, 0, chip(1, half)).wait_send()
-        own_out(half, 1, chip(-1, half)).wait_send()
-
-    @pl.when(c != home)
-    def _():
-        own_query(2, partner).wait_send()
-
-    remote(wo_in.at[other], wo_slot(x, c), wo_own.at[other, 2], wo_recv.at[me], partner).wait_send()
+    take(0, len(arrivals), settle)
+    own_queries(sent)
+    own_outs(sent)
+    lend_outs(sent)
+
+    @pl.when(last)
+    def _():
+        aid_own_query(aid_sent)
+        aid_own_out(aid_sent)
+        steps(1, half_chips + 1, aid_each_query, aid_settle)
+        steps(1, half_chips + 1, aid_each_out, aid_settle)
 
 
 def per_device(seqs, sections, tokens, block_order, prompt_lengths, norm_gain, w_query, w_key_value, w_out, sinks):
@@ -466,8 +752,6 @@
     )
     wkv = turned(pair.astype(F32) * gain)
     wo = jnp.pad(w_out[0], ((0, 0), (0, extra))).reshape(w_out.shape[1], 2, padded // 2).transpose(1, 2, 0)
-    tok = jnp.pad(tokens[block_order], ((0, 0), (0, 0), (0, extra)))
-    lengths = prompt_lengths[block_order]
     freq = jnp.exp(jnp.arange(HALF, dtype=F32) * (-2.0 * math.log(THETA) / HEAD_DIM))
     positions = (me // 2) * (2 * rows) + jnp.arange(2 * rows, dtype=jnp.int32)
     angles = freq[:, None] * positions.astype(F32)[None, :]
@@ -484,13 +768,13 @@
             jax.ShapeDtypeStruct((micro, rows, padded), BF16),
             jax.ShapeDtypeStruct((micro, rows, 2 * kv_width), BF16),
         ),
-        in_specs=[vmem] * 7 + [pl.BlockSpec(memory_space=pltpu.SMEM)],
+        in_specs=[vmem] * 7 + [pl.BlockSpec(memory_space=pltpu.SMEM)] * 2,
         out_specs=(pl.BlockSpec(memory_space=pl.ANY), pl.BlockSpec(memory_space=pl.ANY)),
         scratch_shapes=[
             pltpu.VMEM((2 * tiles, cells, TILE), BF16),
             pltpu.VMEM((shards, tiles * TILE, TILE), BF16),
             pltpu.VMEM((micro, padded, 128), BF16),
-            pltpu.VMEM((micro, 128, padded), BF16),
+            pltpu.VMEM((micro, 128, width), BF16),
             pltpu.VMEM((256, 128), F32),
             pltpu.VMEM((cells, 128), F32),
             pltpu.VMEM((cells, 128), BF16),
@@ -501,8 +785,12 @@
             pltpu.VMEM((micro, tiles, TILE, 128), BF16),
             pltpu.VMEM((micro, tiles, 128, TILE), BF16),
             pltpu.VMEM((micro, 128, 128), BF16),
-            dma((shards,)), dma((3,)), dma((shards,)),
-            dma((seqs,)), dma((2, 3)), dma((seqs,)),
+            pltpu.VMEM((1, cells, TILE), BF16),
+            pltpu.VMEM((shards, TILE * tiles // 2, TILE), BF16),
+            dma((3, shards)), dma((3, 3)), dma((3, shards)),
+            dma((2, seqs)), dma((2, 2, 3)), dma((2, seqs)),
+            dma((shards,)), dma((2, shards)), dma((shards,)),
+            dma((seqs,)), dma((2, seqs)), dma((seqs,)),
             dma, dma((2,)),
             dma((micro, tiles)), dma((micro, tiles)),
             dma((micro, tiles)), dma((micro, tiles)),
@@ -514,7 +802,7 @@
         compiler_params=pltpu.CompilerParams(
             collective_id=0, has_side_effects=True, vmem_limit_bytes=50 * 1024 * 1024
         ),
-    )(wq, wkv, wo, tok, jnp.cos(angles), jnp.sin(angles), sink, lengths)
+    )(wq, wkv, wo, tokens, jnp.cos(angles), jnp.sin(angles), sink, prompt_lengths, block_order)
     return hidden[None, :, :, :width], cache[None]
 
 

time: 293 us -> 269 us (0.918)
  Pallas kernels: 283 us -> 261 us
    pallas_call x1, Pallas kernels: 283 us -> 261 us  [per_device(): pl.pallas_call(functools.partial(kernel, seqs, sections, micro, width), o...]
where the time goes in v3:
time: 269 us; the launch traced here: 268 us
  Pallas kernels  261 us (97%)
  other arithmetic  3.26 us (1%)
  local copies, waits for them, and re-layouts  3.18 us (1%)
    pallas_call x1, Pallas kernels, per_device(): pl.pallas_call(functools.partial(kernel, seqs, sections, micro, width), o...  261 us

profile of v3, /device:TPU:1999, one launch (start us, length us, event | category | flops | bytes accessed | tf_op | source)
XLA Modules:
  0.0 268.3 jit_solution(12885948354810100760)
XLA Ops:
  0.6 0.0 copy-start.4
  0.7 0.8 fusion.2
  1.5 0.1 broadcast_in_dim.6.sink_in
  1.5 0.7 reduce
  2.3 0.1 multiply_sine_fusion
  2.4 0.0 copy-start.3
  2.4 1.4 fusion
  3.8 0.2 copy.10
  4.0 0.0 copy-done.4
  4.1 0.0 copy-done.3
  4.1 0.1 dynamic-slice_bitcast_fusion.1
  4.2 0.3 multiply_convert_fusion
  4.4 0.0 copy-start
  4.5 0.0 copy-start.1
  4.5 0.0 copy-start.2
  4.5 0.1 pad.13
  4.5 0.3 copy.11
  4.8 0.8 copy-done
  5.6 0.0 copy-done.1
  5.6 0.0 copy-done.2
  5.6 261.1 %shard_map.95 = (bf16[4,64,1536]{2,1,0:T(8,128)(2,1)S(1)}, bf16[4,64,512]{2,1,0:T(8,128)(2,1)S(1)}) custom-call(bf16[6,128,256]{2,1,0:T(8,128)(2,1)S(1)} %bitcast.21, bf16[6,256,256]{2,1,0:T(8,128)(2,1)S(1)} %bitcast.20, bf16[2,768,128]{2,1,0:T(8,128)(2,1)S(1)} %bitcast.22, bf16[4,64,1440]{2,1,0:T(8,128)(2,1)S(1)} %copy-done, ...), custom_call_target="tpu_custom_call" | custom-call | tf_op jit(solution)/shard_map/pallas_call | solution.py:765
  266.7 0.9 slice_bitcast_fusion
  267.6 0.7 copy.13
  (5 shorter events, 0.1 us)
Async XLA Ops:
  0.6 3.4 %copy-start.4 = (bf16[1,128,1440]{1,2,0:T(8,128)(2,1)S(1)}, bf16[1,128,1440]{1,2,0:T(8,128)(2,1)}, u32[]{:S(2)}) copy-start(bf16[1,128,1440]{1,2,0:T(8,128)(2,1)} %param.14) | copy-start | bytes 1105924
  2.4 1.6 copy-start.3
  4.4 1.1 copy-start
  4.5 1.1 copy-start.1
  4.5 1.1 copy-start.2

commit v4 on v3

--- a/solution.py
+++ b/solution.py
@@ -573,7 +573,6 @@
         @pl.when(x > 0)
         def _():
             kv_copy(slot, 0).wait_recv()
-            kv_copy(slot, 1).wait_recv()
 
         blank = jnp.zeros((HEAD_DIM, 256), BF16)
         ones = jnp.ones((16, 256), BF16)
@@ -586,22 +585,32 @@
             pair = jnp.concatenate([q[128 * p : 128 * p + 64, :], q[128 * p + 64 : 128 * p + 128, :]], 1)
             return dot(all_keys, jnp.concatenate([pair, blank] if p < group else [blank, pair], 0))
 
+        def spread(pairs):
+            raw = [raw_scores(p) for p in pairs]
+            out = []
+            for p, both in zip(pairs, raw):
+                scores = jnp.where(lower_pair, both[:WIN], both[WIN:]) + bias
+                sink = jnp.concatenate([sink_in[2 * p : 2 * p + 1, :], sink_in[2 * p + 1 : 2 * p + 2, :]], 1)
+                top = jnp.maximum(jnp.max(scores, 0, keepdims=True), sink)
+                out.append((jnp.exp2(scores - top).astype(BF16), jnp.exp2(sink - top)))
+            return out
+
+        soft = spread(range(group))
+
+        @pl.when(x > 0)
+        def _():
+            kv_copy(slot, 1).wait_recv()
+
         for g in range(2):
             pairs = range(group * g, group * (g + 1))
-            raw = [raw_scores(p) for p in pairs]
+            if g > 0:
+                soft = spread(pairs)
             values = jnp.concatenate(
                 [kv_own[slot, 1, 64 * g : 64 * g + 64, :], kv_prev[slot, 1, 64 * g : 64 * g + 64, :]], 1
             )
             values = jnp.concatenate([values, ones], 0)
-            mixed = []
-            rests = []
-            for p, both in zip(pairs, raw):
-                scores = jnp.where(lower_pair, both[:WIN], both[WIN:]) + bias
-                sink = jnp.concatenate([sink_in[2 * p : 2 * p + 1, :], sink_in[2 * p + 1 : 2 * p + 2, :]], 1)
-                top = jnp.maximum(jnp.max(scores, 0, keepdims=True), sink)
-                expo = jnp.exp2(scores - top).astype(BF16)
-                mixed.append(dot(values, jnp.concatenate([expo * own_mask, expo * prev_mask], 0)))
-                rests.append(jnp.exp2(sink - top))
+            mixed = [dot(values, jnp.concatenate([expo * own_mask, expo * prev_mask], 0)) for expo, _ in soft]
+            rests = [rest for _, rest in soft]
             for p, mix, rest in zip(pairs, mixed, rests):
                 total = mix[HEAD_DIM : HEAD_DIM + 1, :] + rest
                 context = (mix[:HEAD_DIM, :] * (1.0 / total)).astype(BF16)
@@ -616,12 +625,15 @@
             return dot(wo[ctx_tiles * core + m, TILE * k : TILE * (k + 1), :], ctx[slot, ctx_tile(core, m), :])
 
         early, late = range(ctx_tiles // 2), range(ctx_tiles // 2, ctx_tiles)
-        for m in early:
-            ctx_copy(slot, other, m).wait_recv()
         for k in range(tiles):
             total = part(c, k, 0)
             for m in range(1, ctx_tiles):
                 total = total + part(c, k, m)
+            o_acc[TILE * k : TILE * (k + 1), :] = total
+        for m in early:
+            ctx_copy(slot, other, m).wait_recv()
+        for k in range(tiles):
+            total = o_acc[TILE * k : TILE * (k + 1), :]
             for m in early:
                 total = total + part(other, k, m)
             o_acc[TILE * k : TILE * (k + 1), :] = total
@@ -654,18 +666,18 @@
 
     take(needed, ending, relay)
 
-    @pl.when(~first)
-    def _():
-        project(0)
-
-    attend(0)
-
     @pl.when(first)
     def _():
+        attend(0)
         project(1)
 
     take(ending, len(arrivals), relay)
     finish_outs()
+
+    @pl.when(~first)
+    def _():
+        project(0)
+        attend(0)
 
     def one_slot(slot, carry):
         emit(slot)
@@ -768,7 +780,10 @@
             jax.ShapeDtypeStruct((micro, rows, padded), BF16),
             jax.ShapeDtypeStruct((micro, rows, 2 * kv_width), BF16),
         ),
-        in_specs=[vmem] * 7 + [pl.BlockSpec(memory_space=pltpu.SMEM)] * 2,
+        in_specs=[vmem] * 3
+        + [pl.BlockSpec(memory_space=pl.ANY)]
+        + [vmem] * 3
+        + [pl.BlockSpec(memory_space=pltpu.SMEM)] * 2,
         out_specs=(pl.BlockSpec(memory_space=pl.ANY), pl.BlockSpec(memory_space=pl.ANY)),
         scratch_shapes=[
             pltpu.VMEM((2 * tiles, cells, TILE), BF16),

time: 269 us -> 271 us (level)
  no operation moved by 1% of the time
where the time goes in v4:
time: 271 us
  Pallas kernels  263 us (97%)
  other arithmetic  3.26 us (1%)
  local copies, waits for them, and re-layouts  3.18 us (1%)
    pallas_call x1, Pallas kernels, per_device(): pl.pallas_call(functools.partial(kernel, seqs, sections, micro, width), o...  263 us

profile of v4, /device:TPU:1999, one launch (start us, length us, event | category | flops | bytes accessed | tf_op | source)
XLA Modules:
  0.0 270.7 jit_solution(9696159661619126120)
XLA Ops:
  0.6 0.0 copy-start.4
  0.7 0.8 fusion.2
  1.5 0.1 broadcast_in_dim.6.sink_in
  1.5 0.7 reduce
  2.3 0.1 multiply_sine_fusion
  2.4 0.0 copy-start.3
  2.4 1.4 fusion
  3.8 0.2 copy.10
  4.0 0.0 copy-done.4
  4.1 0.0 copy-done.3
  4.1 0.1 dynamic-slice_bitcast_fusion.1
  4.2 0.3 multiply_convert_fusion
  4.4 0.0 copy-start
  4.5 0.0 copy-start.1
  4.5 0.0 copy-start.2
  4.5 0.1 pad.13
  4.5 0.3 copy.11
  4.8 0.8 copy-done
  5.6 0.0 copy-done.1
  5.6 0.0 copy-done.2
  5.6 263.4 %shard_map.95 = (bf16[4,64,1536]{2,1,0:T(8,128)(2,1)S(1)}, bf16[4,64,512]{2,1,0:T(8,128)(2,1)S(1)}) custom-call(bf16[6,128,256]{2,1,0:T(8,128)(2,1)S(1)} %bitcast.21, bf16[6,256,256]{2,1,0:T(8,128)(2,1)S(1)} %bitcast.20, bf16[2,768,128]{2,1,0:T(8,128)(2,1)S(1)} %bitcast.22, bf16[4,64,1440]{2,1,0:T(8,128)(2,1)S(1)} %copy-done, ...), custom_call_target="tpu_custom_call" | custom-call | tf_op jit(solution)/shard_map/pallas_call | solution.py:777
  269.0 0.9 slice_bitcast_fusion
  270.0 0.7 copy.13
  (5 shorter events, 0.1 us)
Async XLA Ops:
  0.6 3.4 %copy-start.4 = (bf16[1,128,1440]{1,2,0:T(8,128)(2,1)S(1)}, bf16[1,128,1440]{1,2,0:T(8,128)(2,1)}, u32[]{:S(2)}) copy-start(bf16[1,128,1440]{1,2,0:T(8,128)(2,1)} %param.14) | copy-start | bytes 1105924
  2.4 1.6 copy-start.3
  4.4 1.1 copy-start
  4.5 1.1 copy-start.1
  4.5 1.1 copy-start.2

commit v5 on v4

--- a/solution.py
+++ b/solution.py
@@ -666,18 +666,18 @@
 
     take(needed, ending, relay)
 
+    @pl.when(~first)
+    def _():
+        project(0)
+
+    attend(0)
+
     @pl.when(first)
     def _():
-        attend(0)
         project(1)
 
     take(ending, len(arrivals), relay)
     finish_outs()
-
-    @pl.when(~first)
-    def _():
-        project(0)
-        attend(0)
 
     def one_slot(slot, carry):
         emit(slot)
@@ -780,10 +780,7 @@
             jax.ShapeDtypeStruct((micro, rows, padded), BF16),
             jax.ShapeDtypeStruct((micro, rows, 2 * kv_width), BF16),
         ),
-        in_specs=[vmem] * 3
-        + [pl.BlockSpec(memory_space=pl.ANY)]
-        + [vmem] * 3
-        + [pl.BlockSpec(memory_space=pltpu.SMEM)] * 2,
+        in_specs=[vmem] * 7 + [pl.BlockSpec(memory_space=pltpu.SMEM)] * 2,
         out_specs=(pl.BlockSpec(memory_space=pl.ANY), pl.BlockSpec(memory_space=pl.ANY)),
         scratch_shapes=[
             pltpu.VMEM((2 * tiles, cells, TILE), BF16),

time: 271 us -> 264 us (0.974)
  Pallas kernels: 263 us -> 257 us
    pallas_call x1, Pallas kernels: 263 us -> 257 us  [per_device(): pl.pallas_call(functools.partial(kernel, seqs, sections, micro, width), o...]
where the time goes in v5:
time: 264 us
  Pallas kernels  257 us (97%)
  other arithmetic  3.26 us (1%)
  local copies, waits for them, and re-layouts  3.18 us (1%)
    pallas_call x1, Pallas kernels, per_device(): pl.pallas_call(functools.partial(kernel, seqs, sections, micro, width), o...  257 us

profile of v5, /device:TPU:1999, one launch (start us, length us, event | category | flops | bytes accessed | tf_op | source)
XLA Modules:
  0.0 264.2 jit_solution(14096963535299223559)
XLA Ops:
  0.6 0.0 copy-start.4
  0.7 0.8 fusion.2
  1.5 0.1 broadcast_in_dim.6.sink_in
  1.5 0.7 reduce
  2.3 0.1 multiply_sine_fusion
  2.4 0.0 copy-start.3
  2.4 1.4 fusion
  3.8 0.2 copy.10
  4.0 0.0 copy-done.4
  4.1 0.0 copy-done.3
  4.1 0.1 dynamic-slice_bitcast_fusion.1
  4.2 0.3 multiply_convert_fusion
  4.4 0.0 copy-start
  4.5 0.0 copy-start.1
  4.5 0.0 copy-start.2
  4.5 0.1 pad.13
  4.5 0.3 copy.11
  4.8 0.8 copy-done
  5.6 0.0 copy-done.1
  5.6 0.0 copy-done.2
  5.6 257.0 %shard_map.95 = (bf16[4,64,1536]{2,1,0:T(8,128)(2,1)S(1)}, bf16[4,64,512]{2,1,0:T(8,128)(2,1)S(1)}) custom-call(bf16[6,128,256]{2,1,0:T(8,128)(2,1)S(1)} %bitcast.21, bf16[6,256,256]{2,1,0:T(8,128)(2,1)S(1)} %bitcast.20, bf16[2,768,128]{2,1,0:T(8,128)(2,1)S(1)} %bitcast.22, bf16[4,64,1440]{2,1,0:T(8,128)(2,1)S(1)} %copy-done, ...), custom_call_target="tpu_custom_call" | custom-call | tf_op jit(solution)/shard_map/pallas_call | solution.py:777
  262.6 0.9 slice_bitcast_fusion
  263.5 0.7 copy.13
  (5 shorter events, 0.1 us)
Async XLA Ops:
  0.6 3.4 %copy-start.4 = (bf16[1,128,1440]{1,2,0:T(8,128)(2,1)S(1)}, bf16[1,128,1440]{1,2,0:T(8,128)(2,1)}, u32[]{:S(2)}) copy-start(bf16[1,128,1440]{1,2,0:T(8,128)(2,1)} %param.14) | copy-start | bytes 1105924
  2.4 1.6 copy-start.3
  4.4 1.1 copy-start
  4.5 1.1 copy-start.1
  4.5 1.1 copy-start.2
